TPU v7x, 32 devices: a whole 2x2x4 slice. The times are simulated.
32 devices in a mesh: grp: 4 (over z), dev: 8 (over y, x, core).
Axes of the slice: x: 2, y: 2, z: 4, core: 2. Of those that a mesh axis runs over, the one named last changes fastest.
Arguments:
- matrix_tiles: bfloat16 [640, 128, 1024], P(('grp', 'dev')), may hold values from -0.125 to 0.125
- tile_column: int32 [640], P(('grp', 'dev')), may hold values from 0 to 255
- block_counts: int32 [256], P(('grp', 'dev')), may hold values from 1 to 4, as said below
- destination: int32 [256], P(('grp', 'dev')), may hold values from 0 to 7, as said below
- row_bounds: bfloat16 [32768], P(('grp', 'dev')), may hold values from -6 to 6
- dual_start: bfloat16 [32768], P(('grp', 'dev')), may hold values from 0 to 1
- primal_start: float32 [262144], replicated, may hold values from 0 to 0.5
- cost_vector: float32 [262144], replicated, may hold values from -6 to 6
- upper_bound: float32 [262144], replicated, may hold values from 0.5 to 2
Outputs:
- primal_final: float32 [262144], replicated
- dual_final: float32 [32768], P(('grp', 'dev'))
- weight_final: float32 [1], replicated
Inputs may be any that keep to these rules, and one draw needn't show every extreme that they name: `block_counts`: each device's 8 row blocks have 1 to 4 tiles each and 20 at most together; some device has exactly 20 in every draw. `destination`: on every device the 8 entries are each of 0 to 7 once.
All inputs are finite; a program needn't handle non-finite values.
Results may differ from a plain program's by a relative error of at most 0.0015.
Values may be sent and summed in bfloat16 or wider, within the bound.
A program may use at most 128 MiB of HBM per device.

v0:
```python
import functools

import jax
import jax.numpy as jnp
from jax import lax
from jax.experimental import pallas as pl
from jax.experimental.pallas import tpu as pltpu
from jax.sharding import PartitionSpec as P

NCB = 256
ITERS = 3


step_scale = 0.3


def row_products(tile_store, vector_bf, blocks):
    tile_set, tile_cols, owners, live_flags = tile_store
    vector_table = vector_bf.reshape(-1, tile_set.shape[2])
    column_hot = (
        tile_cols[:, None] == jnp.arange(vector_table.shape[0], dtype=jnp.int32)[None, :]
    ).astype(jnp.bfloat16)
    picked = jnp.dot(column_hot, vector_table, preferred_element_type=jnp.float32).astype(
        jnp.bfloat16
    )
    product = jnp.einsum("src,sc->sr", tile_set, picked, preferred_element_type=jnp.float32)
    product = jnp.where(live_flags[:, None], product, 0.0)
    owner_hot = (jnp.arange(blocks, dtype=jnp.int32)[:, None] == owners[None, :]).astype(
        jnp.float32
    )
    return jnp.dot(owner_hot, product, precision=lax.Precision.HIGHEST)


def column_products(tile_store, rows_bf):
    tile_set, tile_cols, owners, live_flags = tile_store
    blocks = rows_bf.shape[0]
    owner_hot = (owners[:, None] == jnp.arange(blocks, dtype=jnp.int32)[None, :]).astype(
        jnp.bfloat16
    )
    picked_rows = jnp.dot(owner_hot, rows_bf, preferred_element_type=jnp.float32).astype(
        jnp.bfloat16
    )
    product = jnp.einsum("src,sr->sc", tile_set, picked_rows, preferred_element_type=jnp.float32)
    product = jnp.where(live_flags[:, None], product, 0.0)
    column_hot = (jnp.arange(NCB, dtype=jnp.int32)[:, None] == tile_cols[None, :]).astype(
        jnp.float32
    )
    return jnp.dot(column_hot, product, precision=lax.Precision.HIGHEST).reshape(-1)


def per_device(
    matrix_tiles,
    tile_column,
    block_counts,
    destination,
    row_bounds,
    dual_start,
    primal_start,
    cost_vector,
    upper_bound,
):
    blocks = block_counts.shape[0]
    rows_per = matrix_tiles.shape[1]
    slot_count = matrix_tiles.shape[0]
    starts = jnp.cumsum(block_counts) - block_counts
    slot_ids = jnp.arange(slot_count, dtype=jnp.int32)
    owners = jnp.sum((starts[None, 1:] <= slot_ids[:, None]).astype(jnp.int32), axis=1)
    bounds_here = row_bounds.reshape(blocks, rows_per)
    dual_here = dual_start.reshape(blocks, rows_per)
    peer_ids = jnp.arange(blocks, dtype=jnp.int32)
    inverse = jnp.sum(
        jnp.where(destination[None, :] == peer_ids[:, None], peer_ids[None, :], 0), axis=1
    )
    tile_store = (matrix_tiles, tile_column, owners, slot_ids < jnp.sum(block_counts))
    bounds = bounds_here.astype(jnp.float32)
    dual_state = dual_here.astype(jnp.float32)
    primal = primal_start
    weight = jnp.ones((), jnp.float32)
    row_image = row_products(tile_store, primal.astype(jnp.bfloat16), blocks)
    for iteration in range(ITERS):
        step_primal = step_scale / weight
        step_dual = step_scale * weight
        partial_value = column_products(tile_store, dual_state.astype(jnp.bfloat16))
        gradient = lax.psum(partial_value, ("grp", "dev"))
        primal_next = jnp.clip(primal - step_primal * (cost_vector - gradient), 0.0, upper_bound)
        change = jnp.sum((primal_next - primal) ** 2)
        next_image = row_products(tile_store, primal_next.astype(jnp.bfloat16), blocks)
        dual_state = jnp.maximum(
            dual_state + step_dual * (bounds - (2.0 * next_image - row_image)), 0.0
        )
        violation_part = jnp.sum(jnp.maximum(bounds - next_image, 0.0) ** 2)
        violation = lax.psum(violation_part, ("grp", "dev"))
        weight = jnp.sqrt(weight * jnp.sqrt((violation + 1e-06) / (change + 1e-06)))
        primal = primal_next
        row_image = next_image
    dual_final = lax.all_to_all(
        dual_state[inverse], "dev", split_axis=0, concat_axis=0, tiled=True
    ).reshape(-1)
    return (primal, dual_final, jnp.reshape(weight, (1,)))


MESH_ID = pl.DeviceIdType.MESH
SPLIT = 4


def tile_split(slot_count):
    main = slot_count // 16 * 16
    return main, (slot_count - main) * SPLIT


def fits(mesh_shape, slot_count, rows_per, width, blocks, column_blocks):
    main, tail = tile_split(slot_count)
    devices = mesh_shape["grp"] * mesh_shape["dev"]
    rows = main + tail
    per_group = 128
    if main == 0 or per_group % main or rows > 96 or slot_count % 4:
        return False
    if tail == 0 or per_group % tail or tail % 16:
        return False
    if (devices * main) % 128 or (devices * tail) % 128:
        return False
    if rows_per != 128 or width % (128 * SPLIT) or blocks != mesh_shape["dev"]:
        return False
    if mesh_shape["dev"] % 2 or column_blocks > 256 or column_blocks % 16:
        return False
    held = slot_count * rows_per * width * 2 + 2 * devices * rows * width * 2
    return held < 30 * 2**20


def fused_kernel(
    n_grp,
    n_dev,
    indices,
    rows_in,
    tiles,
    primal_in,
    cost_in,
    upper_in,
    out_primal,
    out_dual,
    out_weight,
    kv,
    pv,
    cv,
    uv,
    pnow,
    pbf,
    hot,
    buf,
    stat,
    dsend,
    drecv,
    local_sem,
    piece_send,
    piece_recv,
    stat_send,
    stat_recv,
    dual_send,
    dual_recv,
):
    slots, rows_per, width = tiles.shape
    blocks = rows_in.shape[1]
    cols = [indices[k] for k in range(slots)]
    counts = [indices[slots + k] for k in range(blocks)]
    dest = [indices[slots + blocks + k] for k in range(blocks)]
    n_cb = pnow.shape[0]
    n_all = n_grp * n_dev
    n_chip = n_dev // 2
    main, tail = tile_split(slots)
    rest = slots - main
    rows = main + tail
    sub = width // SPLIT
    chunks = width // 128
    g = lax.axis_index("grp")
    d = lax.axis_index("dev")
    core = d % 2
    chip = d // 2
    partner = chip * 2 + (1 - core)
    me = g * n_dev + d
    f32, bf16, i32 = jnp.float32, jnp.bfloat16, jnp.int32

    def remote(src, dst, ssem, rsem, tg, td):
        return pltpu.make_async_remote_copy(
            src_ref=src,
            dst_ref=dst,
            send_sem=ssem,
            recv_sem=rsem,
            device_id={"grp": tg, "dev": td},
            device_id_type=MESH_ID,
        )

    others = [(a, b) for a in range(n_grp) for b in range(n_dev) if a or b]

    def other(a, b):
        return (g + a) % n_grp, (d + b) % n_dev

    barrier = pltpu.get_barrier_semaphore()
    for a, b in others:
        tg, td = other(a, b)
        pl.semaphore_signal(
            barrier, inc=1, device_id={"grp": tg, "dev": td}, device_id_type=MESH_ID
        )
    copies = [
        pltpu.make_async_copy(primal_in, pv, local_sem.at[0]),
        pltpu.make_async_copy(cost_in, cv, local_sem.at[1]),
        pltpu.make_async_copy(upper_in, uv, local_sem.at[2]),
    ]
    part = 4
    parts = slots // part
    for k in range(parts):
        copies.append(
            pltpu.make_async_copy(
                tiles.at[pl.ds(k * part, part)], kv.at[pl.ds(k * part, part)], local_sem.at[3 + k]
            )
        )
    for k in range(parts):
        copies[3 + k].start()
    copies[0].start()
    copies[1].start()
    copies[2].start()

    def slot_of(pos):
        return jnp.where(pos < main, pos, main + (pos - main) % rest)

    starts = [counts[0] * 0]
    for b in range(blocks):
        starts.append(starts[-1] + counts[b])
    total = starts[-1]
    lane = lax.broadcasted_iota(i32, (1, 128), 1)
    lane_slot = jnp.where(lane < rows, slot_of(lane), slots)
    row = lax.broadcasted_iota(i32, (rows, 128), 0)
    row_slot = slot_of(row)
    row_wide = lax.broadcasted_iota(i32, (rows, n_cb), 0)
    wide_slot = slot_of(row_wide)
    stat_row = jnp.full((1, 128), -1.0, f32)
    wide_col = jnp.full((rows, n_cb), -1, i32)
    owner_of = []
    for s in range(slots):
        live_col = jnp.where(s < total, cols[s], -1)
        stat_row = jnp.where(lane_slot == s, live_col.astype(f32), stat_row)
        wide_col = jnp.where(wide_slot == s, live_col, wide_col)
        who = jnp.int32(0)
        for b in range(1, blocks):
            who = who + jnp.where(starts[b] <= s, 1, 0)
        owner_of.append(jnp.where(s < total, who, -1))
    own_hot = jnp.where(
        wide_col == lax.broadcasted_iota(i32, (rows, n_cb), 1), 1.0, 0.0
    ).astype(bf16)
    row_owner = jnp.zeros((rows, 128), i32)
    for b in range(1, blocks):
        row_owner = row_owner + jnp.where(row_slot >= starts[b], 1, 0)
    row_owner = jnp.where(row_slot < total, row_owner, -1)
    block_row = lax.broadcasted_iota(i32, (blocks, 128), 0)
    bounds = rows_in[0]
    dual = rows_in[1]

    stat[0, me] = stat_row
    pl.semaphore_wait(barrier, len(others))

    def send_stat(turn):
        sent = []
        for k, (a, b) in enumerate(others):
            tg, td = other(a, b)
            copy = remote(
                stat.at[turn, me],
                stat.at[turn, me],
                stat_send.at[turn, k],
                stat_recv.at[turn, me],
                tg,
                td,
            )
            copy.start()
            sent.append(copy)
        return sent

    def wait_stat(turn):
        for a, b in others:
            tg, td = other(a, b)
            src = tg * n_dev + td
            remote(
                stat.at[turn, src],
                stat.at[turn, src],
                stat_send.at[turn, 0],
                stat_recv.at[turn, src],
                tg,
                td,
            ).wait_recv()

    pending = send_stat(0)

    def row_image_of():
        picked = jnp.dot(own_hot, pbf[...], preferred_element_type=f32).astype(bf16)
        chosen = jnp.zeros((rows, rows_per), f32)
        for s in range(0, slots, 2):
            pair = kv[s : s + 2].reshape(2 * rows_per, width)
            both = lax.dot_general(
                picked, pair, (((1,), (1,)), ((), ())), preferred_element_type=f32
            )
            chosen = jnp.where(row == s, both[:, :rows_per], chosen)
            chosen = jnp.where(row == s + 1, both[:, rows_per:], chosen)
        image = jnp.zeros((blocks, rows_per), f32)
        for s in range(slots):
            image = image + jnp.where(block_row == owner_of[s], chosen[s : s + 1, :], 0.0)
        return image

    def write_piece(p, dual_now, loading):
        spread = jnp.zeros((rows, rows_per), f32)
        for b in range(blocks):
            spread = jnp.where(row_owner == b, dual_now[b : b + 1, :], spread)
        total_piece = jnp.zeros((rows, width), f32)
        for s in range(0, slots, 2):
            if loading and s % part == 0:
                copies[3 + s // part].wait()
            left = jnp.concatenate(
                [
                    jnp.where(row_slot == s, spread, 0.0),
                    jnp.where(row_slot == s + 1, spread, 0.0),
                ],
                axis=1,
            ).astype(bf16)
            pair = kv[s : s + 2].reshape(2 * rows_per, width)
            total_piece = total_piece + jnp.dot(left, pair, preferred_element_type=f32)
        quarter = lax.broadcasted_iota(i32, (tail, sub), 0) // rest
        ends = jnp.zeros((tail, sub), f32)
        for q in range(SPLIT):
            part_q = total_piece[:, q * sub : (q + 1) * sub]
            buf[p, me, q * main : (q + 1) * main, :] = part_q[:main].astype(bf16)
            ends = jnp.where(quarter == q, part_q[main:], ends)
        buf[p, me, SPLIT * main : SPLIT * main + tail, :] = ends.astype(bf16)

    def exchange(p, middle, later):
        sent = []

        def send(slot, tg, td):
            copy = remote(
                buf.at[p, slot],
                buf.at[p, slot],
                piece_send.at[len(sent)],
                piece_recv.at[p, slot],
                tg,
                td,
            )
            copy.start()
            sent.append(copy)

        def arrived(slot):
            remote(
                buf.at[p, slot],
                buf.at[p, slot],
                piece_send.at[0],
                piece_recv.at[p, slot],
                g,
                partner,
            ).wait_recv()

        def plane(slot):
            for k in range(1, n_chip):
                send(slot, g, ((chip + k) % n_chip) * 2 + core)
            send(slot, g, partner)

        for a in range(1, n_grp):
            send(me, (g + a) % n_grp, d)
        plane(me)
        middle()
        order = sorted(range(1, n_grp), key=lambda a: min(a, n_grp - a))
        for a in order:
            slot = ((g + a) % n_grp) * n_dev + d
            arrived(slot)
            plane(slot)
        later()
        for a in [0] + order:
            for k in range(1, n_chip):
                slot = ((g + a) % n_grp) * n_dev + ((chip + k) % n_chip) * 2 + core
                arrived(slot)
                send(slot, g, partner)
        for a in [0] + order:
            for k in range(n_chip):
                arrived(((g + a) % n_grp) * n_dev + ((chip + k) % n_chip) * 2 + (1 - core))
        return sent

    def build_hot():
        wait_stat(0)
        block_of = lax.broadcasted_iota(i32, (n_cb, 128), 0).astype(f32)
        for base, size, start in ((0, main, 0), (main, tail, n_all * main)):
            per = 128 // size
            for group in range(n_all // per):
                line = jnp.full((1, 128), -1.0, f32)
                for k in range(per):
                    shift = (k * size - base) % 128
                    source = stat[0, group * per + k]
                    moved = source if shift == 0 else pltpu.roll(source, shift, 1)
                    line = jnp.where(lane // size == k, moved, line)
                match = jnp.where(block_of == line, 1.0, 0.0)
                if base == 0:
                    hot[:, group * 128 : (group + 1) * 128] = match.astype(bf16)
                else:
                    for q in range(SPLIT):
                        at = start + q * n_all * tail + group * 128
                        keep = jnp.where((lane % size) // rest == q, match, 0.0)
                        hot[:, at : at + 128] = keep.astype(bf16)

    weight = jnp.ones((1, 1), f32)
    change = None
    image = None
    for it in range(ITERS):
        p = it % 2
        write_piece(p, dual, it == 0)
        if it == 0:

            images = []

            def first():
                copies[0].wait()
                for j in range(chunks):
                    value = pv[pl.ds(j, n_cb, stride=chunks), :]
                    pnow[:, j * 128 : (j + 1) * 128] = value
                    pbf[:, j * 128 : (j + 1) * 128] = value.astype(bf16)
                build_hot()

            def second():
                images.append(row_image_of())
                copies[1].wait()
                copies[2].wait()

            sent = exchange(p, first, second)
            image = images[0]
        else:
            sent = exchange(p, lambda: None, lambda: None)
            wait_stat(it)
            violation = jnp.sum(stat[it], axis=0)[:, 127:128]
            weight = jnp.sqrt(weight * jnp.sqrt((violation + 1e-06) / (change + 1e-06)))
        tau = step_scale / weight
        ends = buf[p, :, SPLIT * main :, :].reshape(n_all * tail, sub)
        moved_sum = jnp.zeros((8, 128), f32)
        for q in range(SPLIT):
            body = buf[p, :, q * main : (q + 1) * main, :].reshape(n_all * main, sub)
            at = n_all * main + q * n_all * tail
            grad = jnp.dot(hot[:, : n_all * main], body, preferred_element_type=f32)
            grad = grad + jnp.dot(
                hot[:, at : at + n_all * tail], ends, preferred_element_type=f32
            )
            for h in range(sub // 128):
                j = q * (sub // 128) + h
                here = pl.ds(j, n_cb, stride=chunks)
                span = slice(j * 128, (j + 1) * 128)
                old = pnow[:, span]
                stepped = old - tau * (cv[here, :] - grad[:, h * 128 : (h + 1) * 128])
                new = jnp.minimum(jnp.maximum(stepped, 0.0), uv[here, :])
                gap = new - old
                moved_sum = moved_sum + jnp.sum((gap * gap).reshape(n_cb // 8, 8, 128), axis=0)
                pnow[:, span] = new
                pbf[:, span] = new.astype(bf16)
                if it == ITERS - 1:
                    pv[here, :] = new
        if it == ITERS - 1:
            leaving = pltpu.make_async_copy(pv, out_primal, local_sem.at[0])
            leaving.start()
        change = jnp.sum(moved_sum, axis=(0, 1), keepdims=True)
        next_image = row_image_of()
        sigma = step_scale * weight
        dual = jnp.maximum(dual + sigma * (bounds - (2.0 * next_image - image)), 0.0)
        short = jnp.maximum(bounds - next_image, 0.0)
        image = next_image
        stat[it + 1, me] = jnp.where(
            lane == 127, jnp.sum(short * short, axis=(0, 1), keepdims=True), 0.0
        )
        for copy in pending:
            copy.wait_send()
        for copy in sent:
            copy.wait_send()
        pending = send_stat(it + 1)

    for e in range(n_dev):
        line = jnp.zeros((1, rows_per), f32)
        for k in range(blocks):
            line = jnp.where(dest[k] == e, dual[k : k + 1, :], line)
        dsend[e] = line
    sent = []
    for k in range(1, n_dev):
        td = (d + k) % n_dev
        copy = remote(dsend.at[td], drecv.at[d], dual_send.at[k], dual_recv.at[d], g, td)
        copy.start()
        sent.append(copy)
    drecv[d] = dsend[d]
    wait_stat(ITERS)
    violation = jnp.sum(stat[ITERS], axis=0)[:, 127:128]
    weight = jnp.sqrt(weight * jnp.sqrt((violation + 1e-06) / (change + 1e-06)))
    out_weight[...] = jnp.broadcast_to(weight, (1, 128))
    for k in range(1, n_dev):
        src = (d + k) % n_dev
        remote(dsend.at[src], drecv.at[src], dual_send.at[k], dual_recv.at[src], g, src).wait_recv()
    out_dual[...] = drecv[...]
    leaving.wait()
    for copy in pending:
        copy.wait_send()
    for copy in sent:
        copy.wait_send()


def fused_device(mesh_shape, *args):
    tiles, cols, counts, dest, row_bounds, dual_start, primal, cost, upper = args
    slots, rows_per, width = tiles.shape
    blocks = counts.shape[0]
    column_blocks = primal.shape[0] // width
    if not fits(mesh_shape, slots, rows_per, width, blocks, column_blocks):
        return per_device(*args)
    n_grp, n_dev = mesh_shape["grp"], mesh_shape["dev"]
    n_all = n_grp * n_dev
    main, tail = tile_split(slots)
    rows_in = (
        jnp.stack([row_bounds, dual_start]).astype(jnp.float32).reshape(2, blocks, rows_per)
    )
    flat = (primal.shape[0] // 128, 128)
    f32, bf16 = jnp.float32, jnp.bfloat16
    vmem = pl.BlockSpec(memory_space=pltpu.VMEM)
    smem = pl.BlockSpec(memory_space=pltpu.SMEM)
    far = pl.BlockSpec(memory_space=pltpu.HBM)
    sends = (n_grp - 1) + n_grp * (n_dev // 2) + n_grp * (n_dev // 2 - 1)
    out_primal, out_dual, out_weight = pl.pallas_call(
        functools.partial(fused_kernel, n_grp, n_dev),
        name="pdhg_fused",
        out_shape=(
            jax.ShapeDtypeStruct(flat, f32),
            jax.ShapeDtypeStruct((n_dev, 1, rows_per), f32),
            jax.ShapeDtypeStruct((1, 128), f32),
        ),
        in_specs=[smem, vmem, far, far, far, far],
        out_specs=(far, vmem, vmem),
        scratch_shapes=[
            pltpu.VMEM((slots, rows_per, width), bf16),
            pltpu.VMEM(flat, f32),
            pltpu.VMEM(flat, f32),
            pltpu.VMEM(flat, f32),
            pltpu.VMEM((column_blocks, width), f32),
            pltpu.VMEM((column_blocks, width), bf16),
            pltpu.VMEM((column_blocks, n_all * (main + SPLIT * tail)), bf16),
            pltpu.VMEM((2, n_all, SPLIT * main + tail, width // SPLIT), bf16),
            pltpu.VMEM((ITERS + 1, n_all, 1, 128), f32),
            pltpu.VMEM((n_dev, 1, rows_per), f32),
            pltpu.VMEM((n_dev, 1, rows_per), f32),
            pltpu.SemaphoreType.DMA((3 + slots // 4,)),
            pltpu.SemaphoreType.DMA((sends,)),
            pltpu.SemaphoreType.DMA((2, n_all)),
            pltpu.SemaphoreType.DMA((ITERS + 1, n_all)),
            pltpu.SemaphoreType.DMA((ITERS + 1, n_all)),
            pltpu.SemaphoreType.DMA((n_dev,)),
            pltpu.SemaphoreType.DMA((n_dev,)),
        ],
        compiler_params=pltpu.CompilerParams(
            collective_id=0, has_side_effects=True, vmem_limit_bytes=65 * 10**6
        ),
    )(
        jnp.concatenate([cols, counts, dest]),
        rows_in,
        tiles,
        primal.reshape(flat),
        cost.reshape(flat),
        upper.reshape(flat),
    )
    return out_primal.reshape(-1), out_dual.reshape(-1), out_weight[0, :1]


def solution(mesh):
    in_specs = (
        P(("grp", "dev"), None, None),
        P(("grp", "dev")),
        P(("grp", "dev")),
        P(("grp", "dev")),
        P(("grp", "dev")),
        P(("grp", "dev")),
        P(),
        P(),
        P(),
    )
    out_specs = (P(), P(("grp", "dev")), P())
    return jax.shard_map(
        functools.partial(fused_device, dict(mesh.shape)),
        mesh=mesh,
        in_specs=in_specs,
        out_specs=out_specs,
        check_vma=False,
    )
```

profile of v0, /device:TPU:0, one launch (start us, length us, event | category | flops | bytes accessed | tf_op | source)
XLA Modules:
  0.0 75.6 jit_solution(4752829533367166003)
XLA Ops:
  0.6 1.3 %pad_add_fusion.indices = s32[36]{0:T(128)} fusion(s32[8]{0:T(128)} %param.12, s32[8]{0:T(128)} %param.11, s32[20]{0:T(128)} %param.10), kind=kLoop, calls=%fused_computation.1 | loop fusion | flops 72 | bytes 288 | tf_op jit(solution)/shard_map/concatenate | solution.py:553
  1.9 1.3 %maximum_convert_fusion.rows_in = f32[2,8,128]{2,1,0:T(8,128)} fusion(bf16[1,8,128]{2,1,0:T(8,128)(2,1)} %bitcast.14, bf16[1,8,128]{2,1,0:T(8,128)(2,1)} %bitcast.15), kind=kLoop, calls=%fused_computation | loop fusion | flops 4096 | bytes 12288 | tf_op jit(solution)/shard_map/convert_element_type | solution.py:511
  3.2 67.1 %pdhg_fused.1 = (f32[2048,128]{1,0:T(8,128)}, f32[8,1,128]{2,1,0:T(1,128)}, f32[1,128]{1,0:T(1,128)}) custom-call(s32[36]{0:T(128)} %pad_add_fusion.indices, f32[2,8,128]{2,1,0:T(8,128)} %maximum_convert_fusion.rows_in, bf16[20,128,1024]{2,1,0:T(8,128)(2,1)} %tiles.1, f32[2048,128]{1,0:T(8,128)} %bitcast.9, f32[2048,128]{1,0:T(8,128)} %bitcast.10, ...), custom_call_target="tpu_custom_call" | custom-call | tf_op jit(solution)/shard_map/pdhg_fused/pallas_call | solution.py:519
  70.3 2.3 %copy.15 = f32[262144]{0:T(1024)} copy(f32[262144]{0:T(1024)} %bitcast.12) | data formatting | bytes 2097152
  72.6 1.3 %copy.16 = f32[1024]{0:T(1024)} copy(f32[1024]{0:T(1024)} %bitcast.13) | data formatting | bytes 8192
where the time goes:
time: 75.9 us; the launch traced here: 75.6 us
  Pallas kernels  67.1 us (88%)
  local copies, waits for them, and re-layouts  3.53 us (5%)
  other arithmetic  2.57 us (3%)
  between operations  2.4 us (3%)
    pallas_call x1, Pallas kernels, fused_device(): pl.pallas_call(functools.partial(fused_kernel, n_grp, n_dev), name='pdhg_...  67.1 us
    unnamed x2, local copies, waits for them, and re-layouts  3.53 us

commit v1 on v0

v1 whole, which is shorter than its diff:
```python
import functools

import jax
import jax.numpy as jnp
from jax import lax
from jax.experimental import pallas as pl
from jax.experimental.pallas import tpu as pltpu
from jax.sharding import PartitionSpec as P

NCB = 256
ITERS = 3


step_scale = 0.3


def row_products(tile_store, vector_bf, blocks):
    tile_set, tile_cols, owners, live_flags = tile_store
    vector_table = vector_bf.reshape(-1, tile_set.shape[2])
    column_hot = (
        tile_cols[:, None] == jnp.arange(vector_table.shape[0], dtype=jnp.int32)[None, :]
    ).astype(jnp.bfloat16)
    picked = jnp.dot(column_hot, vector_table, preferred_element_type=jnp.float32).astype(
        jnp.bfloat16
    )
    product = jnp.einsum("src,sc->sr", tile_set, picked, preferred_element_type=jnp.float32)
    product = jnp.where(live_flags[:, None], product, 0.0)
    owner_hot = (jnp.arange(blocks, dtype=jnp.int32)[:, None] == owners[None, :]).astype(
        jnp.float32
    )
    return jnp.dot(owner_hot, product, precision=lax.Precision.HIGHEST)


def column_products(tile_store, rows_bf):
    tile_set, tile_cols, owners, live_flags = tile_store
    blocks = rows_bf.shape[0]
    owner_hot = (owners[:, None] == jnp.arange(blocks, dtype=jnp.int32)[None, :]).astype(
        jnp.bfloat16
    )
    picked_rows = jnp.dot(owner_hot, rows_bf, preferred_element_type=jnp.float32).astype(
        jnp.bfloat16
    )
    product = jnp.einsum("src,sr->sc", tile_set, picked_rows, preferred_element_type=jnp.float32)
    product = jnp.where(live_flags[:, None], product, 0.0)
    column_hot = (jnp.arange(NCB, dtype=jnp.int32)[:, None] == tile_cols[None, :]).astype(
        jnp.float32
    )
    return jnp.dot(column_hot, product, precision=lax.Precision.HIGHEST).reshape(-1)


def per_device(
    matrix_tiles,
    tile_column,
    block_counts,
    destination,
    row_bounds,
    dual_start,
    primal_start,
    cost_vector,
    upper_bound,
):
    blocks = block_counts.shape[0]
    rows_per = matrix_tiles.shape[1]
    slot_count = matrix_tiles.shape[0]
    starts = jnp.cumsum(block_counts) - block_counts
    slot_ids = jnp.arange(slot_count, dtype=jnp.int32)
    owners = jnp.sum((starts[None, 1:] <= slot_ids[:, None]).astype(jnp.int32), axis=1)
    bounds_here = row_bounds.reshape(blocks, rows_per)
    dual_here = dual_start.reshape(blocks, rows_per)
    peer_ids = jnp.arange(blocks, dtype=jnp.int32)
    inverse = jnp.sum(
        jnp.where(destination[None, :] == peer_ids[:, None], peer_ids[None, :], 0), axis=1
    )
    tile_store = (matrix_tiles, tile_column, owners, slot_ids < jnp.sum(block_counts))
    bounds = bounds_here.astype(jnp.float32)
    dual_state = dual_here.astype(jnp.float32)
    primal = primal_start
    weight = jnp.ones((), jnp.float32)
    row_image = row_products(tile_store, primal.astype(jnp.bfloat16), blocks)
    for iteration in range(ITERS):
        step_primal = step_scale / weight
        step_dual = step_scale * weight
        partial_value = column_products(tile_store, dual_state.astype(jnp.bfloat16))
        gradient = lax.psum(partial_value, ("grp", "dev"))
        primal_next = jnp.clip(primal - step_primal * (cost_vector - gradient), 0.0, upper_bound)
        change = jnp.sum((primal_next - primal) ** 2)
        next_image = row_products(tile_store, primal_next.astype(jnp.bfloat16), blocks)
        dual_state = jnp.maximum(
            dual_state + step_dual * (bounds - (2.0 * next_image - row_image)), 0.0
        )
        violation_part = jnp.sum(jnp.maximum(bounds - next_image, 0.0) ** 2)
        violation = lax.psum(violation_part, ("grp", "dev"))
        weight = jnp.sqrt(weight * jnp.sqrt((violation + 1e-06) / (change + 1e-06)))
        primal = primal_next
        row_image = next_image
    dual_final = lax.all_to_all(
        dual_state[inverse], "dev", split_axis=0, concat_axis=0, tiled=True
    ).reshape(-1)
    return (primal, dual_final, jnp.reshape(weight, (1,)))


MESH_ID = pl.DeviceIdType.MESH
LANES = 128
TILE = 4


def fits(mesh_shape, slots, rows_per, width, blocks, column_blocks):
    n_grp, n_dev = mesh_shape["grp"], mesh_shape["dev"]
    n_chip = n_dev // 2
    if n_dev % 2 or n_chip & (n_chip - 1) or width != n_dev * LANES:
        return False
    if rows_per != LANES or blocks != n_dev or blocks != 8 or slots > 32:
        return False
    if slots % 4 or (n_grp * n_dev * slots) % LANES or column_blocks % LANES:
        return False
    held = slots * rows_per * width * 2 + column_blocks * width * 4 * 5
    return held < 30 * 2**20


def split_kernel(
    n_grp,
    n_dev,
    cols_in,
    counts_in,
    dest_in,
    bounds_in,
    dual_in,
    tiles,
    primal_in,
    cost_in,
    upper_in,
    out_primal,
    out_dual,
    out_weight,
    kv,
    pv,
    cv,
    uv,
    cs,
    us,
    pnow,
    pbf,
    hot,
    hot_back,
    asend,
    abuf,
    bsend,
    bbuf,
    stat,
    fbuf,
    dsend,
    drecv,
    tile_sem,
    local_sem,
    out_sem,
    a_send,
    a_recv,
    b_send,
    b_recv,
    stat_send,
    stat_recv,
    f_send,
    f_recv,
    p_send,
    p_recv,
    dual_send,
    dual_recv,
):
    slots, rows_per, width = tiles.shape
    blocks = bounds_in.shape[0]
    n_cb = pnow.shape[0]
    n_all = n_grp * n_dev
    n_chip = n_dev // 2
    span = 2 * LANES
    packs = slots // TILE
    f32, bf16, i32 = jnp.float32, jnp.bfloat16, jnp.int32
    g = lax.axis_index("grp")
    d = lax.axis_index("dev")
    core = d % 2
    chip = d // 2
    twin = 1 - core
    partner = chip * 2 + twin
    me = g * n_dev + d

    def remote(src, dst, ssem, rsem, tg, td):
        return pltpu.make_async_remote_copy(
            src_ref=src,
            dst_ref=dst,
            send_sem=ssem,
            recv_sem=rsem,
            device_id={"grp": tg, "dev": td},
            device_id_type=MESH_ID,
        )

    def bytes_of(ref, ssem, rsem):
        return remote(ref, ref, ssem, rsem, g, partner)

    others = [(a, b) for a in range(n_grp) for b in range(n_dev) if a or b]

    def other(a, b):
        return (g + a) % n_grp, (d + b) % n_dev

    def chunk(u):
        return pl.ds(pl.multiple_of((chip ^ u) * span, span), span)

    barrier = pltpu.get_barrier_semaphore()
    for a, b in others:
        tg, td = other(a, b)
        pl.semaphore_signal(
            barrier, inc=1, device_id={"grp": tg, "dev": td}, device_id_type=MESH_ID
        )
    order = [u for u in range(n_chip - 1, 0, -1)] + [0]
    part = 4
    for u in order:
        for k in range(0, slots, part):
            pltpu.make_async_copy(
                tiles.at[pl.ds(k, part), :, chunk(u)],
                kv.at[pl.ds(k, part), :, chunk(u)],
                tile_sem.at[u],
            ).start()
    copies = [
        pltpu.make_async_copy(primal_in, pv, local_sem.at[0]),
        pltpu.make_async_copy(cost_in, cv, local_sem.at[1]),
        pltpu.make_async_copy(upper_in, uv, local_sem.at[2]),
    ]
    for copy in copies:
        copy.start()

    cols = [cols_in[k] for k in range(slots)]
    counts = [counts_in[k] for k in range(blocks)]
    dest = [dest_in[k] for k in range(blocks)]
    starts = [counts[0] * 0]
    for b in range(blocks):
        starts.append(starts[-1] + counts[b])
    total = starts[-1]
    live = [jnp.where(s < total, cols[s], -1) for s in range(slots)]
    lane = lax.broadcasted_iota(i32, (1, LANES), 1)
    turn = (me * slots) % LANES
    place = jnp.where(lane < turn, lane - turn + LANES, lane - turn)
    stat_row = jnp.full((1, LANES), -1.0, f32)
    for s in range(slots):
        stat_row = jnp.where(place == s, live[s].astype(f32), stat_row)
    stat[0, me] = stat_row
    rows = 32
    row = lax.broadcasted_iota(i32, (rows, LANES), 0)
    row_owner = jnp.zeros((rows, LANES), i32)
    for b in range(1, blocks):
        row_owner = row_owner + jnp.where(row >= starts[b], 1, 0)
    row_owner = jnp.where(row < total, row_owner, -1)
    own_lane = lax.broadcasted_iota(i32, (blocks, slots), 1)
    own_row = lax.broadcasted_iota(i32, (blocks, slots), 0)
    first = jnp.zeros((blocks, slots), i32)
    last = jnp.zeros((blocks, slots), i32)
    for b in range(blocks):
        first = jnp.where(own_row == b, starts[b], first)
        last = jnp.where(own_row == b, starts[b + 1], last)
    owner_hot = jnp.where((own_lane >= first) & (own_lane < last), 1.0, 0.0).astype(bf16)
    slot_lane = lax.broadcasted_iota(i32, (rows_per, slots), 1)
    bounds = bounds_in[...].astype(f32)
    dual = dual_in[...].astype(f32)

    def pieces(it, dual_now, before):
        spread = jnp.zeros((rows, rows_per), f32)
        for b in range(blocks):
            spread = jnp.where(row_owner == b, dual_now[b : b + 1, :], spread)
        left = [
            jnp.concatenate(
                [jnp.where(row == s, spread, 0.0), jnp.where(row == s + 1, spread, 0.0)],
                axis=1,
            ).astype(bf16)
            for s in range(0, slots, 2)
        ]
        for u in order:
            before(u)
            whole = jnp.zeros((rows, span), f32)
            for s in range(0, slots, 2):
                pair = kv[s : s + 2, :, chunk(u)].reshape(2 * rows_per, span)
                whole = whole + jnp.dot(left[s // 2], pair, preferred_element_type=f32)
            halves = [
                whole[:slots, h * LANES : (h + 1) * LANES].astype(bf16).reshape(packs, TILE, LANES)
                for h in range(2)
            ]
            for h in range(2):
                asend[it, u, h] = halves[h]
            if u == 0:
                abuf[it, pl.ds(me * packs, packs)] = jnp.where(core == 0, halves[0], halves[1])

    def send_pieces(it, u):
        def send(src, tg, td):
            remote(
                src,
                abuf.at[it, pl.ds(me * packs, packs)],
                a_send.at[it],
                a_recv.at[it],
                tg,
                td,
            ).start()

        for a in range(n_grp - 1, 0, -1):
            for h in range(2):
                send(asend.at[it, u, h], (g + a) % n_grp, (chip ^ u) * 2 + h)
        if u:
            for h in range(2):
                send(asend.at[it, u, h], g, (chip ^ u) * 2 + h)
        else:
            send(asend.at[it, 0, twin], g, partner)

    def send_stat(turn_no):
        for a, b in others:
            tg, td = other(a, b)
            remote(
                stat.at[turn_no, me],
                stat.at[turn_no, me],
                stat_send.at[turn_no],
                stat_recv.at[turn_no],
                tg,
                td,
            ).start()

    def stat_bytes(turn_no):
        return bytes_of(
            stat.at[turn_no, pl.ds(0, n_all - 1)], stat_send.at[turn_no], stat_recv.at[turn_no]
        )

    def piece_bytes(it):
        return bytes_of(
            abuf.at[it, pl.ds(0, (n_all - 1) * packs)], a_send.at[it], a_recv.at[it]
        )

    def image_part(acc, picked, lanes):
        for s in range(0, slots, 4):
            block = kv[s : s + 4, :, lanes].reshape(4 * rows_per, span)
            out = lax.dot_general(
                block, picked, (((1,), (1,)), ((), ())), preferred_element_type=f32
            )
            for k in range(4):
                here = out[k * rows_per : (k + 1) * rows_per]
                acc = jnp.where(slot_lane == s + k, acc + here, acc)
        return acc

    def image_of(acc):
        high = acc.astype(bf16)
        rest = acc - high.astype(f32)
        mid = rest.astype(bf16)
        low = (rest - mid.astype(f32)).astype(bf16)
        image = jnp.zeros((blocks, rows_per), f32)
        for term in (high, mid, low):
            image = image + lax.dot_general(
                owner_hot, term, (((1,), (1,)), ((), ())), preferred_element_type=f32
            )
        return image

    def no_image():
        return jnp.zeros((rows_per, slots), f32)

    def first_image():
        copies[0].wait()
        for j in range(n_dev):
            value = pv[pl.ds(j, n_cb, stride=n_dev), :]
            pbf[:, j * LANES : (j + 1) * LANES] = value.astype(bf16)
        pnow[...] = pv[pl.ds(d, n_cb, stride=n_dev), :]
        wide = lax.broadcasted_iota(i32, (rows, n_cb), 0)
        wide_col = jnp.full((rows, n_cb), -1, i32)
        for s in range(slots):
            wide_col = jnp.where(wide == s, live[s], wide_col)
        own_hot = jnp.where(
            wide_col == lax.broadcasted_iota(i32, (rows, n_cb), 1), 1.0, 0.0
        ).astype(bf16)
        picked = jnp.dot(own_hot, pbf[...], preferred_element_type=f32).astype(bf16)[:slots]
        acc = no_image()
        for c in range(n_chip):
            lanes = slice(c * span, (c + 1) * span)
            acc = image_part(acc, picked[:, lanes], lanes)
        return image_of(acc)

    def build_hot():
        stat_bytes(0).wait_recv()
        block_of = lax.broadcasted_iota(i32, (n_cb, LANES), 0).astype(f32)
        for t in range(n_all * slots // LANES):
            line = jnp.full((1, LANES), -1.0, f32)
            for k in range(n_all):
                low, high = k * slots - t * LANES, (k + 1) * slots - t * LANES
                if high > 0 and low < LANES:
                    line = jnp.where((lane >= low) & (lane < high), stat[0, k], line)
            hot[:, t * LANES : (t + 1) * LANES] = jnp.where(block_of == line, 1.0, 0.0).astype(bf16)
        back = n_dev * slots
        back_row = lax.broadcasted_iota(i32, (back, LANES), 0)
        back_lane = lax.broadcasted_iota(i32, (back, LANES), 1)
        back_dev, back_slot = back_row // slots, back_row % slots
        found = jnp.zeros((back, LANES), f32)
        for u in range(n_chip):
            for h in range(2):
                src = g * n_dev + (chip ^ u) * 2 + h
                shift = (src * slots) % LANES
                at = jnp.where(back_lane < shift, back_lane - shift + LANES, back_lane - shift)
                hit = (back_dev == u * 2 + h) & (at == back_slot)
                found = jnp.where(hit, stat[0, src] + 1.0, found)
        wanted = jnp.sum(found, axis=1, keepdims=True) - 1.0
        lane_cb = lax.broadcasted_iota(i32, (back, n_cb), 1).astype(f32)
        hot_back[...] = jnp.where(wanted == lane_cb, 1.0, 0.0).astype(bf16)

    def load_slices():
        copies[1].wait()
        copies[2].wait()
        cs[...] = cv[pl.ds(d, n_cb, stride=n_dev), :]
        us[...] = uv[pl.ds(d, n_cb, stride=n_dev), :]

    weight = jnp.ones((1, 1), f32)
    image = None
    for it in range(ITERS):
        if it == 0:

            def ready(u):
                pltpu.make_async_copy(
                    tiles.at[:, :, chunk(u)], kv.at[:, :, chunk(u)], tile_sem.at[u]
                ).wait()

            pieces(it, dual, ready)
            pl.semaphore_wait(barrier, len(others))
            send_stat(0)
            for u in order:
                send_pieces(it, u)
            image = first_image()
            load_slices()
            build_hot()
        else:
            sent_before = []

            def flow(u):
                if sent_before:
                    send_pieces(it, sent_before[-1])
                sent_before.append(u)

            pieces(it, dual, flow)
            send_pieces(it, sent_before[-1])
            stat_bytes(it).wait_recv()
            violation = jnp.sum(stat[it], axis=0)[:, LANES - 1 :]
            change = jnp.sum(stat[it, 0:n_dev], axis=0)[:, :1]
            weight = jnp.sqrt(weight * jnp.sqrt((violation + 1e-06) / (change + 1e-06)))
        tau = step_scale / weight
        piece_bytes(it).wait_recv()
        grad = jnp.dot(
            hot[...],
            abuf.at[it].reshape(n_all * slots, LANES)[...],
            preferred_element_type=f32,
        )
        old = pnow[...]
        new = jnp.minimum(jnp.maximum(old - tau * (cs[...] - grad), 0.0), us[...])
        back = jnp.dot(hot_back[...], new.astype(bf16), preferred_element_type=f32)
        back = back.astype(bf16).reshape(n_chip, 2, packs, TILE, LANES)
        bsend[it] = back
        bbuf[it, 0, core] = jnp.where(core == 0, back[0, 0], back[0, 1])

        def send_back(src, dst, u, td):
            remote(src, dst, b_send.at[it], b_recv.at[it, u], g, td).start()

        for u in order[:-1]:
            for h in range(2):
                send_back(
                    bsend.at[it, u, h], bbuf.at[it, u, core], u, (chip ^ u) * 2 + h
                )
        send_back(bsend.at[it, 0, twin], bbuf.at[it, 0, core], 0, partner)
        gap = new - old
        moved = jnp.sum(gap * gap, axis=(0, 1), keepdims=True)
        if it < ITERS - 1:
            pnow[...] = new
        else:
            fbuf[0] = new
            for u in order[:-1]:
                remote(
                    fbuf.at[0], fbuf.at[u], f_send.at[0], f_recv.at[u], g, (chip ^ u) * 2 + core
                ).start()
            remote(fbuf.at[0], out_primal.at[d], p_send.at[0], p_recv.at[0], g, partner).start()
            pltpu.make_async_copy(fbuf.at[0], out_primal.at[d], out_sem.at[0]).start()

        acc = no_image()
        for u in range(n_chip):
            one = bbuf.at[it, 0, 0] if u == 0 else bbuf.at[it, u]
            bytes_of(one, b_send.at[it], b_recv.at[it, u]).wait_recv()
            picked = jnp.concatenate(
                [bbuf[it, u, h].reshape(slots, LANES) for h in range(2)], axis=1
            )
            acc = image_part(acc, picked, chunk(u))
        next_image = image_of(acc)
        sigma = step_scale * weight
        dual = jnp.maximum(dual + sigma * (bounds - (2.0 * next_image - image)), 0.0)
        short = jnp.maximum(bounds - next_image, 0.0)
        image = next_image
        missed = jnp.sum(short * short, axis=(0, 1), keepdims=True)
        stat[it + 1, me] = jnp.where(lane < LANES // 2, moved, missed)
        send_stat(it + 1)

    for e in range(n_dev):
        line = jnp.zeros((1, rows_per), f32)
        for k in range(blocks):
            line = jnp.where(dest[k] == e, dual[k : k + 1, :], line)
        dsend[e] = line
    for k in range(1, n_dev):
        td = (d + k) % n_dev
        remote(dsend.at[td], drecv.at[d], dual_send.at[0], dual_recv.at[0], g, td).start()
    drecv[d] = dsend[d]
    for u in range(1, n_chip):
        bytes_of(fbuf.at[u], f_send.at[0], f_recv.at[u]).wait_recv()
        src = (chip ^ u) * 2 + core
        remote(fbuf.at[u], out_primal.at[src], p_send.at[0], p_recv.at[0], g, partner).start()
        pltpu.make_async_copy(fbuf.at[u], out_primal.at[src], out_sem.at[0]).start()
    bytes_of(drecv.at[pl.ds(0, n_dev - 1)], dual_send.at[0], dual_recv.at[0]).wait_recv()
    out_dual[...] = drecv[...]
    stat_bytes(ITERS).wait_recv()
    violation = jnp.sum(stat[ITERS], axis=0)[:, LANES - 1 :]
    change = jnp.sum(stat[ITERS, 0:n_dev], axis=0)[:, :1]
    weight = jnp.sqrt(weight * jnp.sqrt((violation + 1e-06) / (change + 1e-06)))
    out_weight[...] = jnp.broadcast_to(weight, (1, LANES))
    for it in range(ITERS):
        piece_bytes(it).wait_send()
        bytes_of(
            bbuf.at[it, pl.ds(0, n_chip - 1)], b_send.at[it], b_recv.at[it, 0]
        ).wait_send()
        bytes_of(bbuf.at[it, 0, 0], b_send.at[it], b_recv.at[it, 0]).wait_send()
    for turn_no in range(ITERS + 1):
        stat_bytes(turn_no).wait_send()
    bytes_of(drecv.at[pl.ds(0, n_dev - 1)], dual_send.at[0], dual_recv.at[0]).wait_send()
    bytes_of(fbuf.at[pl.ds(0, n_chip - 1)], f_send.at[0], f_recv.at[0]).wait_send()
    bytes_of(fbuf, p_send.at[0], p_recv.at[0]).wait_send()
    bytes_of(fbuf, p_send.at[0], p_recv.at[0]).wait_recv()
    pltpu.make_async_copy(fbuf, out_primal.at[pl.ds(0, n_chip)], out_sem.at[0]).wait()


def split_device(mesh_shape, *args):
    tiles, cols, counts, dest, row_bounds, dual_start, primal, cost, upper = args
    slots, rows_per, width = tiles.shape
    blocks = counts.shape[0]
    n_cb = primal.shape[0] // width
    if not fits(mesh_shape, slots, rows_per, width, blocks, n_cb):
        return per_device(*args)
    n_grp, n_dev = mesh_shape["grp"], mesh_shape["dev"]
    n_all, n_chip = n_grp * n_dev, n_dev // 2
    packs = slots // TILE
    flat = (primal.shape[0] // LANES, LANES)
    f32, bf16 = jnp.float32, jnp.bfloat16
    vmem = pl.BlockSpec(memory_space=pltpu.VMEM)
    smem = pl.BlockSpec(memory_space=pltpu.SMEM)
    far = pl.BlockSpec(memory_space=pltpu.HBM)
    dma = pltpu.SemaphoreType.DMA
    out_primal, out_dual, out_weight = pl.pallas_call(
        functools.partial(split_kernel, n_grp, n_dev),
        name="pdhg_split",
        out_shape=(
            jax.ShapeDtypeStruct((n_dev, n_cb, LANES), f32),
            jax.ShapeDtypeStruct((n_dev, 1, rows_per), f32),
            jax.ShapeDtypeStruct((1, LANES), f32),
        ),
        in_specs=[smem, smem, smem, vmem, vmem, far, far, far, far],
        out_specs=(far, vmem, vmem),
        scratch_shapes=[
            pltpu.VMEM((slots, rows_per, width), bf16),
            pltpu.VMEM(flat, f32),
            pltpu.VMEM(flat, f32),
            pltpu.VMEM(flat, f32),
            pltpu.VMEM((n_cb, LANES), f32),
            pltpu.VMEM((n_cb, LANES), f32),
            pltpu.VMEM((n_cb, LANES), f32),
            pltpu.VMEM((n_cb, width), bf16),
            pltpu.VMEM((n_cb, n_all * slots), bf16),
            pltpu.VMEM((n_dev * slots, n_cb), bf16),
            pltpu.VMEM((ITERS, n_chip, 2, packs, TILE, LANES), bf16),
            pltpu.VMEM((ITERS, n_all * packs, TILE, LANES), bf16),
            pltpu.VMEM((ITERS, n_chip, 2, packs, TILE, LANES), bf16),
            pltpu.VMEM((ITERS, n_chip, 2, packs, TILE, LANES), bf16),
            pltpu.VMEM((ITERS + 1, n_all, 1, LANES), f32),
            pltpu.VMEM((n_chip, n_cb, LANES), f32),
            pltpu.VMEM((n_dev, 1, rows_per), f32),
            pltpu.VMEM((n_dev, 1, rows_per), f32),
            dma((n_chip,)),
            dma((3,)),
            dma((1,)),
            dma((ITERS,)),
            dma((ITERS,)),
            dma((ITERS,)),
            dma((ITERS, n_chip)),
            dma((ITERS + 1,)),
            dma((ITERS + 1,)),
            dma((1,)),
            dma((n_chip,)),
            dma((1,)),
            dma((1,)),
            dma((1,)),
            dma((1,)),
        ],
        compiler_params=pltpu.CompilerParams(
            collective_id=0, has_side_effects=True, vmem_limit_bytes=50 * 10**6
        ),
    )(
        cols,
        counts,
        dest,
        row_bounds.reshape(blocks, rows_per),
        dual_start.reshape(blocks, rows_per),
        tiles,
        primal.reshape(flat),
        cost.reshape(flat),
        upper.reshape(flat),
    )
    primal_final = out_primal.transpose(1, 0, 2).reshape(-1)
    return primal_final, out_dual.reshape(-1), out_weight[0, :1]


def solution(mesh):
    in_specs = (
        P(("grp", "dev"), None, None),
        P(("grp", "dev")),
        P(("grp", "dev")),
        P(("grp", "dev")),
        P(("grp", "dev")),
        P(("grp", "dev")),
        P(),
        P(),
        P(),
    )
    out_specs = (P(), P(("grp", "dev")), P())
    return jax.shard_map(
        functools.partial(split_device, dict(mesh.shape)),
        mesh=mesh,
        in_specs=in_specs,
        out_specs=out_specs,
        check_vma=False,
    )
```

time: 75.9 us -> 58.9 us (0.78)
  Pallas kernels: 67.1 us -> 47.6 us
  local copies, waits for them, and re-layouts: 3.53 us -> 9.17 us
  other arithmetic: 2.57 us -> 0 us
    pallas_call x1, Pallas kernels: 67.1 us -> 47.6 us  [split_device(): pl.pallas_call(functools.partial(split_kernel, n_grp, n_dev), name='pdhg_...]
    unnamed x2 -> x17, local copies, waits for them, and re-layouts: 3.53 us -> 7.59 us
    transpose x0 -> x1, local copies, waits for them, and re-layouts: none -> 1.58 us  [split_device(): primal_final = out_primal.transpose(1, 0, 2).reshape(-1)]
    convert_element_type x1 -> x0, other arithmetic: 1.3 us -> none  [fused_device(): jnp.stack([row_bounds, dual_start]).astype(jnp.float32)]
    concatenate x1 -> x0, other arithmetic: 1.27 us -> none  [fused_device(): jnp.concatenate([cols, counts, dest])]
where the time goes in v1:
time: 58.9 us; the launch traced here: 58.6 us
  Pallas kernels  47.6 us (81%)
  local copies, waits for them, and re-layouts  9.17 us (16%)
  between operations  1.82 us (3%)
    pallas_call x1, Pallas kernels, split_device(): pl.pallas_call(functools.partial(split_kernel, n_grp, n_dev), name='pdhg_...  47.6 us
    unnamed x17, local copies, waits for them, and re-layouts  7.59 us
    transpose x1, local copies, waits for them, and re-layouts, split_device(): primal_final = out_primal.transpose(1, 0, 2).reshape(-1)  1.58 us

profile of v1, /device:TPU:0, one launch (start us, length us, event | category | flops | bytes accessed | tf_op | source)
XLA Modules:
  0.0 58.6 jit_solution(8751797451897896932)
XLA Ops:
  0.6 0.0 copy-start
  0.6 1.2 %copy-done = f32[262144]{0:T(1024)S(1)} copy-done((f32[262144]{0:T(1024)S(1)}, f32[262144]{0:T(1024)}, u32[]{:S(2)}) %copy-start) | copy-done | bytes 1048600
  1.9 0.0 copy-start.1
  1.9 1.2 %copy-done.1 = f32[262144]{0:T(1024)S(1)} copy-done((f32[262144]{0:T(1024)S(1)}, f32[262144]{0:T(1024)}, u32[]{:S(2)}) %copy-start.1) | copy-done | bytes 1048600
  3.1 0.0 copy-start.2
  3.1 1.2 %copy-done.2 = f32[262144]{0:T(1024)S(1)} copy-done((f32[262144]{0:T(1024)S(1)}, f32[262144]{0:T(1024)}, u32[]{:S(2)}) %copy-start.2) | copy-done | bytes 1048600
  4.3 0.0 copy-start.3
  4.3 0.7 %copy-done.3 = bf16[1024]{0:T(1024)(128)(2,1)S(1)} copy-done((bf16[1024]{0:T(1024)(128)(2,1)S(1)}, bf16[1024]{0:T(1024)(128)(2,1)}, u32[]{:S(2)}) %copy-start.3) | copy-done | bytes 2072
  5.0 0.0 copy-start.4
  5.0 0.7 %copy-done.4 = bf16[1024]{0:T(1024)(128)(2,1)S(1)} copy-done((bf16[1024]{0:T(1024)(128)(2,1)S(1)}, bf16[1024]{0:T(1024)(128)(2,1)}, u32[]{:S(2)}) %copy-start.4) | copy-done | bytes 2072
  5.7 0.0 copy-start.5
  5.7 0.7 %copy-done.5 = s32[20]{0:T(128)S(1)} copy-done((s32[20]{0:T(128)S(1)}, s32[20]{0:T(128)}, u32[]{:S(2)}) %copy-start.5) | copy-done | bytes 104
  6.3 0.0 copy-start.6
  6.3 0.7 %copy-done.6 = s32[8]{0:T(128)S(1)} copy-done((s32[8]{0:T(128)S(1)}, s32[8]{0:T(128)}, u32[]{:S(2)}) %copy-start.6) | copy-done | bytes 56
  7.0 0.0 copy-start.7
  7.0 0.7 %copy-done.7 = s32[8]{0:T(128)S(1)} copy-done((s32[8]{0:T(128)S(1)}, s32[8]{0:T(128)}, u32[]{:S(2)}) %copy-start.7) | copy-done | bytes 56
  7.6 47.6 %pdhg_split.1 = (f32[8,256,128]{2,1,0:T(8,128)S(1)}, f32[8,1,128]{2,1,0:T(1,128)S(1)}, f32[1,128]{1,0:T(1,128)S(1)}) custom-call(s32[20]{0:T(128)S(1)} %copy-done.5, s32[8]{0:T(128)S(1)} %copy-done.6, s32[8]{0:T(128)S(1)} %copy-done.7, bf16[8,128]{1,0:T(8,128)(2,1)S(1)} %bitcast.17, bf16[8,128]{1,0:T(8,128)(2,1)S(1)} %bitcast.18, ...), custom_call_target="tpu_custom_call" | custom-call | tf_op jit(solution)/shard_map/pdhg_split/pallas_call | solution.py:545
  55.2 1.6 %copy.14 = f32[256,8,128]{2,1,0:T(8,128)} copy(f32[256,8,128]{2,0,1:T(8,128)S(1)} %bitcast.12) | data formatting | bytes 2097152 | tf_op jit(solution)/shard_map/transpose | solution.py:604
  56.8 0.6 %copy.17 = f32[1024]{0:T(1024)} copy(f32[1024]{0:T(1024)S(1)} %bitcast.16) | data formatting | bytes 8192
Async XLA Ops:
  0.6 1.2 %copy-start = (f32[262144]{0:T(1024)S(1)}, f32[262144]{0:T(1024)}, u32[]{:S(2)}) copy-start(f32[262144]{0:T(1024)} %param.15) | copy-start | bytes 3145732
  1.9 1.2 %copy-start.1 = (f32[262144]{0:T(1024)S(1)}, f32[262144]{0:T(1024)}, u32[]{:S(2)}) copy-start(f32[262144]{0:T(1024)} %param.16) | copy-start | bytes 3145732
  3.1 1.2 %copy-start.2 = (f32[262144]{0:T(1024)S(1)}, f32[262144]{0:T(1024)}, u32[]{:S(2)}) copy-start(f32[262144]{0:T(1024)} %param.17) | copy-start | bytes 3145732
  4.3 0.7 %copy-start.3 = (bf16[1024]{0:T(1024)(128)(2,1)S(1)}, bf16[1024]{0:T(1024)(128)(2,1)}, u32[]{:S(2)}) copy-start(bf16[1024]{0:T(1024)(128)(2,1)} %param.13) | copy-start | bytes 6148
  5.0 0.7 %copy-start.4 = (bf16[1024]{0:T(1024)(128)(2,1)S(1)}, bf16[1024]{0:T(1024)(128)(2,1)}, u32[]{:S(2)}) copy-start(bf16[1024]{0:T(1024)(128)(2,1)} %param.14) | copy-start | bytes 6148
  5.7 0.7 %copy-start.5 = (s32[20]{0:T(128)S(1)}, s32[20]{0:T(128)}, u32[]{:S(2)}) copy-start(s32[20]{0:T(128)} %cols_in.1) | copy-start | bytes 244
  6.3 0.7 %copy-start.6 = (s32[8]{0:T(128)S(1)}, s32[8]{0:T(128)}, u32[]{:S(2)}) copy-start(s32[8]{0:T(128)} %counts_in.1) | copy-start | bytes 100
  7.0 0.7 %copy-start.7 = (s32[8]{0:T(128)S(1)}, s32[8]{0:T(128)}, u32[]{:S(2)}) copy-start(s32[8]{0:T(128)} %dest_in.1) | copy-start | bytes 100

commit v2 on v1

--- a/solution.py
+++ b/solution.py
@@ -150,8 +150,14 @@
     fbuf,
     dsend,
     drecv,
+    cols_at,
+    counts_at,
+    dest_at,
+    bounds_at,
+    dual_at,
     tile_sem,
     local_sem,
+    small_sem,
     out_sem,
     a_send,
     a_recv,
@@ -209,6 +215,20 @@
         pl.semaphore_signal(
             barrier, inc=1, device_id={"grp": tg, "dev": td}, device_id_type=MESH_ID
         )
+    small = [
+        pltpu.make_async_copy(src, dst, small_sem.at[k])
+        for k, (src, dst) in enumerate(
+            (
+                (cols_in, cols_at),
+                (counts_in, counts_at),
+                (dest_in, dest_at),
+                (bounds_in, bounds_at),
+                (dual_in, dual_at),
+            )
+        )
+    ]
+    for copy in small:
+        copy.start()
     order = [u for u in range(n_chip - 1, 0, -1)] + [0]
     part = 4
     for u in order:
@@ -226,9 +246,11 @@
     for copy in copies:
         copy.start()
 
-    cols = [cols_in[k] for k in range(slots)]
-    counts = [counts_in[k] for k in range(blocks)]
-    dest = [dest_in[k] for k in range(blocks)]
+    for copy in small:
+        copy.wait()
+    cols = [cols_at[k] for k in range(slots)]
+    counts = [counts_at[k] for k in range(blocks)]
+    dest = [dest_at[k] for k in range(blocks)]
     starts = [counts[0] * 0]
     for b in range(blocks):
         starts.append(starts[-1] + counts[b])
@@ -256,8 +278,8 @@
         last = jnp.where(own_row == b, starts[b + 1], last)
     owner_hot = jnp.where((own_lane >= first) & (own_lane < last), 1.0, 0.0).astype(bf16)
     slot_lane = lax.broadcasted_iota(i32, (rows_per, slots), 1)
-    bounds = bounds_in[...].astype(f32)
-    dual = dual_in[...].astype(f32)
+    bounds = bounds_at[...].astype(f32)
+    dual = dual_at[...].astype(f32)
 
     def pieces(it, dual_now, before):
         spread = jnp.zeros((rows, rows_per), f32)
@@ -539,7 +561,6 @@
     flat = (primal.shape[0] // LANES, LANES)
     f32, bf16 = jnp.float32, jnp.bfloat16
     vmem = pl.BlockSpec(memory_space=pltpu.VMEM)
-    smem = pl.BlockSpec(memory_space=pltpu.SMEM)
     far = pl.BlockSpec(memory_space=pltpu.HBM)
     dma = pltpu.SemaphoreType.DMA
     out_primal, out_dual, out_weight = pl.pallas_call(
@@ -550,7 +571,7 @@
             jax.ShapeDtypeStruct((n_dev, 1, rows_per), f32),
             jax.ShapeDtypeStruct((1, LANES), f32),
         ),
-        in_specs=[smem, smem, smem, vmem, vmem, far, far, far, far],
+        in_specs=[far] * 9,
         out_specs=(far, vmem, vmem),
         scratch_shapes=[
             pltpu.VMEM((slots, rows_per, width), bf16),
@@ -571,8 +592,14 @@
             pltpu.VMEM((n_chip, n_cb, LANES), f32),
             pltpu.VMEM((n_dev, 1, rows_per), f32),
             pltpu.VMEM((n_dev, 1, rows_per), f32),
+            pltpu.SMEM((slots,), jnp.int32),
+            pltpu.SMEM((blocks,), jnp.int32),
+            pltpu.SMEM((blocks,), jnp.int32),
+            pltpu.VMEM((blocks, rows_per), bf16),
+            pltpu.VMEM((blocks, rows_per), bf16),
             dma((n_chip,)),
             dma((3,)),
+            dma((5,)),
             dma((1,)),
             dma((ITERS,)),
             dma((ITERS,)),

time: 58.9 us -> 58.3 us (0.990)
  Pallas kernels: 47.6 us -> 47 us
    pallas_call x1, Pallas kernels: 47.6 us -> 47 us  [split_device(): pl.pallas_call(functools.partial(split_kernel, n_grp, n_dev), name='pdhg_...]
where the time goes in v2:
time: 58.3 us; the launch traced here: 57.9 us
  Pallas kernels  47 us (81%)
  local copies, waits for them, and re-layouts  9.17 us (16%)
  between operations  1.82 us (3%)
    pallas_call x1, Pallas kernels, split_device(): pl.pallas_call(functools.partial(split_kernel, n_grp, n_dev), name='pdhg_...  47 us
    unnamed x17, local copies, waits for them, and re-layouts  7.59 us
    transpose x1, local copies, waits for them, and re-layouts, split_device(): primal_final = out_primal.transpose(1, 0, 2).reshape(-1)  1.58 us

profile of v2, /device:TPU:0, one launch (start us, length us, event | category | flops | bytes accessed | tf_op | source)
XLA Modules:
  0.0 57.9 jit_solution(13667330670589283737)
XLA Ops:
  0.6 0.0 copy-start
  0.6 1.2 %copy-done = f32[262144]{0:T(1024)S(1)} copy-done((f32[262144]{0:T(1024)S(1)}, f32[262144]{0:T(1024)}, u32[]{:S(2)}) %copy-start) | copy-done | bytes 1048600
  1.9 0.0 copy-start.1
  1.9 1.2 %copy-done.1 = f32[262144]{0:T(1024)S(1)} copy-done((f32[262144]{0:T(1024)S(1)}, f32[262144]{0:T(1024)}, u32[]{:S(2)}) %copy-start.1) | copy-done | bytes 1048600
  3.1 0.0 copy-start.2
  3.1 1.2 %copy-done.2 = f32[262144]{0:T(1024)S(1)} copy-done((f32[262144]{0:T(1024)S(1)}, f32[262144]{0:T(1024)}, u32[]{:S(2)}) %copy-start.2) | copy-done | bytes 1048600
  4.3 0.0 copy-start.3
  4.3 0.7 %copy-done.3 = bf16[1024]{0:T(1024)(128)(2,1)S(1)} copy-done((bf16[1024]{0:T(1024)(128)(2,1)S(1)}, bf16[1024]{0:T(1024)(128)(2,1)}, u32[]{:S(2)}) %copy-start.3) | copy-done | bytes 2072
  5.0 0.0 copy-start.4
  5.0 0.7 %copy-done.4 = bf16[1024]{0:T(1024)(128)(2,1)S(1)} copy-done((bf16[1024]{0:T(1024)(128)(2,1)S(1)}, bf16[1024]{0:T(1024)(128)(2,1)}, u32[]{:S(2)}) %copy-start.4) | copy-done | bytes 2072
  5.7 0.0 copy-start.5
  5.7 0.7 %copy-done.5 = s32[20]{0:T(128)S(1)} copy-done((s32[20]{0:T(128)S(1)}, s32[20]{0:T(128)}, u32[]{:S(2)}) %copy-start.5) | copy-done | bytes 104
  6.3 0.0 copy-start.6
  6.3 0.7 %copy-done.6 = s32[8]{0:T(128)S(1)} copy-done((s32[8]{0:T(128)S(1)}, s32[8]{0:T(128)}, u32[]{:S(2)}) %copy-start.6) | copy-done | bytes 56
  7.0 0.0 copy-start.7
  7.0 0.7 %copy-done.7 = s32[8]{0:T(128)S(1)} copy-done((s32[8]{0:T(128)S(1)}, s32[8]{0:T(128)}, u32[]{:S(2)}) %copy-start.7) | copy-done | bytes 56
  7.6 47.0 %pdhg_split.1 = (f32[8,256,128]{2,1,0:T(8,128)S(1)}, f32[8,1,128]{2,1,0:T(1,128)S(1)}, f32[1,128]{1,0:T(1,128)S(1)}) custom-call(s32[20]{0:T(128)S(1)} %copy-done.5, s32[8]{0:T(128)S(1)} %copy-done.6, s32[8]{0:T(128)S(1)} %copy-done.7, bf16[8,128]{1,0:T(8,128)(2,1)S(1)} %bitcast.17, bf16[8,128]{1,0:T(8,128)(2,1)S(1)} %bitcast.18, ...), custom_call_target="tpu_custom_call" | custom-call | tf_op jit(solution)/shard_map/pdhg_split/pallas_call | solution.py:566
  54.6 1.6 %copy.14 = f32[256,8,128]{2,1,0:T(8,128)} copy(f32[256,8,128]{2,0,1:T(8,128)S(1)} %bitcast.12) | data formatting | bytes 2097152 | tf_op jit(solution)/shard_map/transpose | solution.py:631
  56.2 0.6 %copy.17 = f32[1024]{0:T(1024)} copy(f32[1024]{0:T(1024)S(1)} %bitcast.16) | data formatting | bytes 8192
Async XLA Ops:
  0.6 1.2 %copy-start = (f32[262144]{0:T(1024)S(1)}, f32[262144]{0:T(1024)}, u32[]{:S(2)}) copy-start(f32[262144]{0:T(1024)} %param.15) | copy-start | bytes 3145732
  1.9 1.2 %copy-start.1 = (f32[262144]{0:T(1024)S(1)}, f32[262144]{0:T(1024)}, u32[]{:S(2)}) copy-start(f32[262144]{0:T(1024)} %param.16) | copy-start | bytes 3145732
  3.1 1.2 %copy-start.2 = (f32[262144]{0:T(1024)S(1)}, f32[262144]{0:T(1024)}, u32[]{:S(2)}) copy-start(f32[262144]{0:T(1024)} %param.17) | copy-start | bytes 3145732
  4.3 0.7 %copy-start.3 = (bf16[1024]{0:T(1024)(128)(2,1)S(1)}, bf16[1024]{0:T(1024)(128)(2,1)}, u32[]{:S(2)}) copy-start(bf16[1024]{0:T(1024)(128)(2,1)} %param.13) | copy-start | bytes 6148
  5.0 0.7 %copy-start.4 = (bf16[1024]{0:T(1024)(128)(2,1)S(1)}, bf16[1024]{0:T(1024)(128)(2,1)}, u32[]{:S(2)}) copy-start(bf16[1024]{0:T(1024)(128)(2,1)} %param.14) | copy-start | bytes 6148
  5.7 0.7 %copy-start.5 = (s32[20]{0:T(128)S(1)}, s32[20]{0:T(128)}, u32[]{:S(2)}) copy-start(s32[20]{0:T(128)} %cols_in.1) | copy-start | bytes 244
  6.3 0.7 %copy-start.6 = (s32[8]{0:T(128)S(1)}, s32[8]{0:T(128)}, u32[]{:S(2)}) copy-start(s32[8]{0:T(128)} %counts_in.1) | copy-start | bytes 100
  7.0 0.7 %copy-start.7 = (s32[8]{0:T(128)S(1)}, s32[8]{0:T(128)}, u32[]{:S(2)}) copy-start(s32[8]{0:T(128)} %dest_in.1) | copy-start | bytes 100

commit v3 on v2

--- a/solution.py
+++ b/solution.py
@@ -615,7 +615,7 @@
             dma((1,)),
         ],
         compiler_params=pltpu.CompilerParams(
-            collective_id=0, has_side_effects=True, vmem_limit_bytes=50 * 10**6
+            collective_id=0, has_side_effects=True, vmem_limit_bytes=65 * 10**6
         ),
     )(
         cols,

time: 58.3 us -> 55.5 us (0.952)
  local copies, waits for them, and re-layouts: 9.17 us -> 4.08 us
  Pallas kernels: 47 us -> 48.8 us
  between operations: 1.82 us -> 2.41 us
    unnamed x17 -> x1, local copies, waits for them, and re-layouts: 7.59 us -> 1.27 us
    pallas_call x1, Pallas kernels: 47 us -> 48.8 us  [split_device(): pl.pallas_call(functools.partial(split_kernel, n_grp, n_dev), name='pdhg_...]
    transpose x1, local copies, waits for them, and re-layouts: 1.58 us -> 2.81 us  [split_device(): primal_final = out_primal.transpose(1, 0, 2).reshape(-1)]
where the time goes in v3:
time: 55.5 us; the launch traced here: 55.3 us
  Pallas kernels  48.8 us (88%)
  local copies, waits for them, and re-layouts  4.08 us (7%)
  between operations  2.41 us (4%)
    pallas_call x1, Pallas kernels, split_device(): pl.pallas_call(functools.partial(split_kernel, n_grp, n_dev), name='pdhg_...  48.8 us
    transpose x1, local copies, waits for them, and re-layouts, split_device(): primal_final = out_primal.transpose(1, 0, 2).reshape(-1)  2.81 us
    unnamed x1, local copies, waits for them, and re-layouts  1.27 us

profile of v3, /device:TPU:0, one launch (start us, length us, event | category | flops | bytes accessed | tf_op | source)
XLA Modules:
  0.0 55.3 jit_solution(5624525788417108527)
XLA Ops:
  0.6 48.8 %pdhg_split.1 = (f32[8,256,128]{2,1,0:T(8,128)}, f32[8,1,128]{2,1,0:T(1,128)}, f32[1,128]{1,0:T(1,128)}) custom-call(s32[20]{0:T(128)} %cols_in.1, s32[8]{0:T(128)} %counts_in.1, s32[8]{0:T(128)} %dest_in.1, bf16[8,128]{1,0:T(8,128)(2,1)} %bitcast.18, bf16[8,128]{1,0:T(8,128)(2,1)} %bitcast.19, bf16[20,128,1024]{2,1,0:T(8,128)(2,1)} %tiles.1, ...), custom_call_target="tpu_custom_call" | custom-call | tf_op jit(solution)/shard_map/pdhg_split/pallas_call | solution.py:566
  49.5 2.8 %copy.14 = f32[256,8,128]{2,1,0:T(8,128)} copy(f32[256,8,128]{2,0,1:T(8,128)} %bitcast.13) | data formatting | bytes 2097152 | tf_op jit(solution)/shard_map/transpose | solution.py:631
  52.3 1.3 %copy.17 = f32[1024]{0:T(1024)} copy(f32[1024]{0:T(1024)} %bitcast.17) | data formatting | bytes 8192

commit v4 on v3

--- a/solution.py
+++ b/solution.py
@@ -107,7 +107,7 @@
 def fits(mesh_shape, slots, rows_per, width, blocks, column_blocks):
     n_grp, n_dev = mesh_shape["grp"], mesh_shape["dev"]
     n_chip = n_dev // 2
-    if n_dev % 2 or n_chip & (n_chip - 1) or width != n_dev * LANES:
+    if n_dev % 2 or n_chip & (n_chip - 1) or n_grp & (n_grp - 1) or width != n_dev * LANES:
         return False
     if rows_per != LANES or blocks != n_dev or blocks != 8 or slots > 32:
         return False
@@ -147,7 +147,6 @@
     bsend,
     bbuf,
     stat,
-    fbuf,
     dsend,
     drecv,
     cols_at,
@@ -158,7 +157,6 @@
     tile_sem,
     local_sem,
     small_sem,
-    out_sem,
     a_send,
     a_recv,
     b_send,
@@ -230,24 +228,29 @@
     for copy in small:
         copy.start()
     order = [u for u in range(n_chip - 1, 0, -1)] + [0]
+    planes = sorted(range(1, n_grp), key=lambda a: (-(a.bit_length()), a))
     part = 4
-    for u in order:
+    group = slots // 4
+
+    def fetch(u):
         for k in range(0, slots, part):
             pltpu.make_async_copy(
                 tiles.at[pl.ds(k, part), :, chunk(u)],
                 kv.at[pl.ds(k, part), :, chunk(u)],
                 tile_sem.at[u],
             ).start()
+
+    fetch(order[0])
     copies = [
         pltpu.make_async_copy(primal_in, pv, local_sem.at[0]),
         pltpu.make_async_copy(cost_in, cv, local_sem.at[1]),
         pltpu.make_async_copy(upper_in, uv, local_sem.at[2]),
     ]
-    for copy in copies:
-        copy.start()
 
     for copy in small:
         copy.wait()
+    for u in order[1:]:
+        fetch(u)
     cols = [cols_at[k] for k in range(slots)]
     counts = [counts_at[k] for k in range(blocks)]
     dest = [dest_at[k] for k in range(blocks)]
@@ -263,12 +266,18 @@
     for s in range(slots):
         stat_row = jnp.where(place == s, live[s].astype(f32), stat_row)
     stat[0, me] = stat_row
-    rows = 32
+    rows = 16
     row = lax.broadcasted_iota(i32, (rows, LANES), 0)
-    row_owner = jnp.zeros((rows, LANES), i32)
-    for b in range(1, blocks):
-        row_owner = row_owner + jnp.where(row >= starts[b], 1, 0)
-    row_owner = jnp.where(row < total, row_owner, -1)
+    split = (slots // 2 + 1) // 2 * 2
+    lead = split % TILE
+    groups = []
+    for low, high, base in ((0, split, 0), (split, slots, split - lead)):
+        slot = row + base
+        owner = jnp.zeros((rows, LANES), i32)
+        for b in range(1, blocks):
+            owner = owner + jnp.where(slot >= starts[b], 1, 0)
+        owner = jnp.where((slot < total) & (slot >= low) & (slot < high), owner, -1)
+        groups.append((low, high, slot, owner))
     own_lane = lax.broadcasted_iota(i32, (blocks, slots), 1)
     own_row = lax.broadcasted_iota(i32, (blocks, slots), 0)
     first = jnp.zeros((blocks, slots), i32)
@@ -282,26 +291,41 @@
     dual = dual_at[...].astype(f32)
 
     def pieces(it, dual_now, before):
-        spread = jnp.zeros((rows, rows_per), f32)
-        for b in range(blocks):
-            spread = jnp.where(row_owner == b, dual_now[b : b + 1, :], spread)
-        left = [
-            jnp.concatenate(
-                [jnp.where(row == s, spread, 0.0), jnp.where(row == s + 1, spread, 0.0)],
-                axis=1,
-            ).astype(bf16)
-            for s in range(0, slots, 2)
-        ]
+        left = {}
+        for low, high, slot, owner in groups:
+            spread = jnp.zeros((rows, rows_per), f32)
+            for b in range(blocks):
+                spread = jnp.where(owner == b, dual_now[b : b + 1, :], spread)
+            for s in range(low, high, 2):
+                left[s] = jnp.concatenate(
+                    [jnp.where(slot == s, spread, 0.0), jnp.where(slot == s + 1, spread, 0.0)],
+                    axis=1,
+                ).astype(bf16)
         for u in order:
             before(u)
-            whole = jnp.zeros((rows, span), f32)
-            for s in range(0, slots, 2):
-                pair = kv[s : s + 2, :, chunk(u)].reshape(2 * rows_per, span)
-                whole = whole + jnp.dot(left[s // 2], pair, preferred_element_type=f32)
+            sums = []
+            for low, high, _, _ in groups:
+                whole = jnp.zeros((rows, span), f32)
+                for s in range(low, high, 2):
+                    pair = kv[s : s + 2, :, chunk(u)].reshape(2 * rows_per, span)
+                    whole = whole + jnp.dot(left[s], pair, preferred_element_type=f32)
+                sums.append(whole)
+            head, tail = sums[0], sums[1]
+            even = split - lead
+            joined = [head[:even]]
+            if lead:
+                joined.append(head[even : even + TILE] + tail[:TILE])
+                joined.append(tail[TILE : slots - even])
+            else:
+                joined.append(tail[: slots - even])
             halves = [
-                whole[:slots, h * LANES : (h + 1) * LANES].astype(bf16).reshape(packs, TILE, LANES)
+                [
+                    x[:, h * LANES : (h + 1) * LANES].astype(bf16).reshape(-1, TILE, LANES)
+                    for x in joined
+                ]
                 for h in range(2)
             ]
+            halves = [jnp.concatenate(x, axis=0) for x in halves]
             for h in range(2):
                 asend[it, u, h] = halves[h]
             if u == 0:
@@ -318,9 +342,9 @@
                 td,
             ).start()
 
-        for a in range(n_grp - 1, 0, -1):
+        for a in planes:
             for h in range(2):
-                send(asend.at[it, u, h], (g + a) % n_grp, (chip ^ u) * 2 + h)
+                send(asend.at[it, u, h], g ^ a, (chip ^ u) * 2 + h)
         if u:
             for h in range(2):
                 send(asend.at[it, u, h], g, (chip ^ u) * 2 + h)
@@ -350,12 +374,12 @@
         )
 
     def image_part(acc, picked, lanes):
-        for s in range(0, slots, 4):
-            block = kv[s : s + 4, :, lanes].reshape(4 * rows_per, span)
+        for s in range(0, slots, group):
+            block = kv[s : s + group, :, lanes].reshape(group * rows_per, span)
             out = lax.dot_general(
                 block, picked, (((1,), (1,)), ((), ())), preferred_element_type=f32
             )
-            for k in range(4):
+            for k in range(group):
                 here = out[k * rows_per : (k + 1) * rows_per]
                 acc = jnp.where(slot_lane == s + k, acc + here, acc)
         return acc
@@ -381,12 +405,12 @@
             value = pv[pl.ds(j, n_cb, stride=n_dev), :]
             pbf[:, j * LANES : (j + 1) * LANES] = value.astype(bf16)
         pnow[...] = pv[pl.ds(d, n_cb, stride=n_dev), :]
-        wide = lax.broadcasted_iota(i32, (rows, n_cb), 0)
-        wide_col = jnp.full((rows, n_cb), -1, i32)
+        wide = lax.broadcasted_iota(i32, (32, n_cb), 0)
+        wide_col = jnp.full((32, n_cb), -1, i32)
         for s in range(slots):
             wide_col = jnp.where(wide == s, live[s], wide_col)
         own_hot = jnp.where(
-            wide_col == lax.broadcasted_iota(i32, (rows, n_cb), 1), 1.0, 0.0
+            wide_col == lax.broadcasted_iota(i32, (32, n_cb), 1), 1.0, 0.0
         ).astype(bf16)
         picked = jnp.dot(own_hot, pbf[...], preferred_element_type=f32).astype(bf16)[:slots]
         acc = no_image()
@@ -433,6 +457,9 @@
         if it == 0:
 
             def ready(u):
+                if u == order[-1]:
+                    for copy in copies:
+                        copy.start()
                 pltpu.make_async_copy(
                     tiles.at[:, :, chunk(u)], kv.at[:, :, chunk(u)], tile_sem.at[u]
                 ).wait()
@@ -487,13 +514,19 @@
         if it < ITERS - 1:
             pnow[...] = new
         else:
-            fbuf[0] = new
+            out_primal[d] = new
             for u in order[:-1]:
                 remote(
-                    fbuf.at[0], fbuf.at[u], f_send.at[0], f_recv.at[u], g, (chip ^ u) * 2 + core
+                    out_primal.at[d],
+                    out_primal.at[d],
+                    f_send.at[0],
+                    f_recv.at[u],
+                    g,
+                    (chip ^ u) * 2 + core,
                 ).start()
-            remote(fbuf.at[0], out_primal.at[d], p_send.at[0], p_recv.at[0], g, partner).start()
-            pltpu.make_async_copy(fbuf.at[0], out_primal.at[d], out_sem.at[0]).start()
+            remote(
+                out_primal.at[d], out_primal.at[d], p_send.at[0], p_recv.at[0], g, partner
+            ).start()
 
         acc = no_image()
         for u in range(n_chip):
@@ -522,10 +555,11 @@
         remote(dsend.at[td], drecv.at[d], dual_send.at[0], dual_recv.at[0], g, td).start()
     drecv[d] = dsend[d]
     for u in range(1, n_chip):
-        bytes_of(fbuf.at[u], f_send.at[0], f_recv.at[u]).wait_recv()
         src = (chip ^ u) * 2 + core
-        remote(fbuf.at[u], out_primal.at[src], p_send.at[0], p_recv.at[0], g, partner).start()
-        pltpu.make_async_copy(fbuf.at[u], out_primal.at[src], out_sem.at[0]).start()
+        bytes_of(out_primal.at[src], f_send.at[0], f_recv.at[u]).wait_recv()
+        remote(
+            out_primal.at[src], out_primal.at[src], p_send.at[0], p_recv.at[0], g, partner
+        ).start()
     bytes_of(drecv.at[pl.ds(0, n_dev - 1)], dual_send.at[0], dual_recv.at[0]).wait_recv()
     out_dual[...] = drecv[...]
     stat_bytes(ITERS).wait_recv()
@@ -542,10 +576,9 @@
     for turn_no in range(ITERS + 1):
         stat_bytes(turn_no).wait_send()
     bytes_of(drecv.at[pl.ds(0, n_dev - 1)], dual_send.at[0], dual_recv.at[0]).wait_send()
-    bytes_of(fbuf.at[pl.ds(0, n_chip - 1)], f_send.at[0], f_recv.at[0]).wait_send()
-    bytes_of(fbuf, p_send.at[0], p_recv.at[0]).wait_send()
-    bytes_of(fbuf, p_send.at[0], p_recv.at[0]).wait_recv()
-    pltpu.make_async_copy(fbuf, out_primal.at[pl.ds(0, n_chip)], out_sem.at[0]).wait()
+    bytes_of(out_primal.at[pl.ds(0, n_chip - 1)], f_send.at[0], f_recv.at[0]).wait_send()
+    bytes_of(out_primal.at[pl.ds(0, n_chip)], p_send.at[0], p_recv.at[0]).wait_send()
+    bytes_of(out_primal.at[pl.ds(0, n_chip)], p_send.at[0], p_recv.at[0]).wait_recv()
 
 
 def split_device(mesh_shape, *args):
@@ -567,12 +600,12 @@
         functools.partial(split_kernel, n_grp, n_dev),
         name="pdhg_split",
         out_shape=(
-            jax.ShapeDtypeStruct((n_dev, n_cb, LANES), f32),
-            jax.ShapeDtypeStruct((n_dev, 1, rows_per), f32),
-            jax.ShapeDtypeStruct((1, LANES), f32),
+            pltpu.VMEM((n_dev, n_cb, LANES), f32),
+            pltpu.VMEM((n_dev, 1, rows_per), f32),
+            pltpu.VMEM((1, LANES), f32),
         ),
         in_specs=[far] * 9,
-        out_specs=(far, vmem, vmem),
+        out_specs=(vmem, vmem, vmem),
         scratch_shapes=[
             pltpu.VMEM((slots, rows_per, width), bf16),
             pltpu.VMEM(flat, f32),
@@ -589,7 +622,6 @@
             pltpu.VMEM((ITERS, n_chip, 2, packs, TILE, LANES), bf16),
             pltpu.VMEM((ITERS, n_chip, 2, packs, TILE, LANES), bf16),
             pltpu.VMEM((ITERS + 1, n_all, 1, LANES), f32),
-            pltpu.VMEM((n_chip, n_cb, LANES), f32),
             pltpu.VMEM((n_dev, 1, rows_per), f32),
             pltpu.VMEM((n_dev, 1, rows_per), f32),
             pltpu.SMEM((slots,), jnp.int32),
@@ -600,7 +632,6 @@
             dma((n_chip,)),
             dma((3,)),
             dma((5,)),
-            dma((1,)),
             dma((ITERS,)),
             dma((ITERS,)),
             dma((ITERS,)),
@@ -618,15 +649,20 @@
             collective_id=0, has_side_effects=True, vmem_limit_bytes=65 * 10**6
         ),
     )(
-        cols,
-        counts,
-        dest,
-        row_bounds.reshape(blocks, rows_per),
-        dual_start.reshape(blocks, rows_per),
-        tiles,
-        primal.reshape(flat),
-        cost.reshape(flat),
-        upper.reshape(flat),
+        *(
+            pltpu.with_memory_space_constraint(x, pltpu.HBM)
+            for x in (
+                cols,
+                counts,
+                dest,
+                row_bounds.reshape(blocks, rows_per),
+                dual_start.reshape(blocks, rows_per),
+                tiles,
+                primal.reshape(flat),
+                cost.reshape(flat),
+                upper.reshape(flat),
+            )
+        )
     )
     primal_final = out_primal.transpose(1, 0, 2).reshape(-1)
     return primal_final, out_dual.reshape(-1), out_weight[0, :1]

time: 55.5 us -> 50.9 us (0.917)
  Pallas kernels: 48.8 us -> 46.7 us
  local copies, waits for them, and re-layouts: 4.08 us -> 2.17 us
  between operations: 2.41 us -> 1.81 us
    pallas_call x1, Pallas kernels: 48.8 us -> 46.7 us  [split_device(): pl.pallas_call(functools.partial(split_kernel, n_grp, n_dev), name='pdhg_...]
    transpose x1, local copies, waits for them, and re-layouts: 2.81 us -> 1.58 us  [split_device(): primal_final = out_primal.transpose(1, 0, 2).reshape(-1)]
    unnamed x1, local copies, waits for them, and re-layouts: 1.27 us -> 0.59 us
where the time goes in v4:
time: 50.9 us; the launch traced here: 50.7 us
  Pallas kernels  46.7 us (92%)
  local copies, waits for them, and re-layouts  2.17 us (4%)
  between operations  1.81 us (4%)
    pallas_call x1, Pallas kernels, split_device(): pl.pallas_call(functools.partial(split_kernel, n_grp, n_dev), name='pdhg_...  46.7 us
    transpose x1, local copies, waits for them, and re-layouts, split_device(): primal_final = out_primal.transpose(1, 0, 2).reshape(-1)  1.58 us

profile of v4, /device:TPU:0, one launch (start us, length us, event | category | flops | bytes accessed | tf_op | source)
XLA Modules:
  0.0 50.7 jit_solution(16944262529107110984)
XLA Ops:
  0.6 46.7 %pdhg_split.1 = (f32[8,256,128]{2,1,0:T(8,128)S(1)}, f32[8,1,128]{2,1,0:T(1,128)S(1)}, f32[1,128]{1,0:T(1,128)S(1)}) custom-call(s32[20]{0:T(128)} %cols_in.1, s32[8]{0:T(128)} %counts_in.1, s32[8]{0:T(128)} %dest_in.1, bf16[8,128]{1,0:T(8,128)(2,1)} %bitcast.19, bf16[8,128]{1,0:T(8,128)(2,1)} %bitcast.20, bf16[20,128,1024]{2,1,0:T(8,128)(2,1)} %tiles.1, ...), custom_call_target="tpu_custom_call" | custom-call | tf_op jit(solution)/shard_map/pdhg_split/pallas_call | solution.py:599
  47.4 1.6 %copy.14 = f32[256,8,128]{2,1,0:T(8,128)} copy(f32[256,8,128]{2,0,1:T(8,128)S(1)} %bitcast.13) | data formatting | bytes 2097152 | tf_op jit(solution)/shard_map/transpose | solution.py:667
  48.9 0.6 %copy.17 = f32[1024]{0:T(1024)} copy(f32[1024]{0:T(1024)S(1)} %bitcast.12) | data formatting | bytes 8192

commit v5 on v4

--- a/solution.py
+++ b/solution.py
@@ -113,7 +113,7 @@
         return False
     if slots % 4 or (n_grp * n_dev * slots) % LANES or column_blocks % LANES:
         return False
-    held = slots * rows_per * width * 2 + column_blocks * width * 4 * 5
+    held = slots * rows_per * width * 4 + column_blocks * width * 4 * 5
     return held < 30 * 2**20
 
 
@@ -133,6 +133,7 @@
     out_dual,
     out_weight,
     kv,
+    kvt,
     pv,
     cv,
     uv,
@@ -229,8 +230,8 @@
         copy.start()
     order = [u for u in range(n_chip - 1, 0, -1)] + [0]
     planes = sorted(range(1, n_grp), key=lambda a: (-(a.bit_length()), a))
+    stages = [[0], [u for u in range(1, n_chip - 1)], [n_chip - 1]]
     part = 4
-    group = slots // 4
 
     def fetch(u):
         for k in range(0, slots, part):
@@ -278,15 +279,8 @@
             owner = owner + jnp.where(slot >= starts[b], 1, 0)
         owner = jnp.where((slot < total) & (slot >= low) & (slot < high), owner, -1)
         groups.append((low, high, slot, owner))
-    own_lane = lax.broadcasted_iota(i32, (blocks, slots), 1)
-    own_row = lax.broadcasted_iota(i32, (blocks, slots), 0)
-    first = jnp.zeros((blocks, slots), i32)
-    last = jnp.zeros((blocks, slots), i32)
-    for b in range(blocks):
-        first = jnp.where(own_row == b, starts[b], first)
-        last = jnp.where(own_row == b, starts[b + 1], last)
-    owner_hot = jnp.where((own_lane >= first) & (own_lane < last), 1.0, 0.0).astype(bf16)
-    slot_lane = lax.broadcasted_iota(i32, (rows_per, slots), 1)
+    block_row = lax.broadcasted_iota(i32, (blocks, rows_per), 0)
+    slot_row = lax.broadcasted_iota(i32, (slots, rows_per), 0)
     bounds = bounds_at[...].astype(f32)
     dual = dual_at[...].astype(f32)
 
@@ -373,31 +367,39 @@
             abuf.at[it, pl.ds(0, (n_all - 1) * packs)], a_send.at[it], a_recv.at[it]
         )
 
-    def image_part(acc, picked, lanes):
-        for s in range(0, slots, group):
-            block = kv[s : s + group, :, lanes].reshape(group * rows_per, span)
-            out = lax.dot_general(
-                block, picked, (((1,), (1,)), ((), ())), preferred_element_type=f32
-            )
-            for k in range(group):
-                here = out[k * rows_per : (k + 1) * rows_per]
-                acc = jnp.where(slot_lane == s + k, acc + here, acc)
-        return acc
+    owners = []
+
+    def find_owners():
+        for k in range(slots):
+            who = jnp.int32(0)
+            for b in range(1, blocks):
+                who = who + jnp.where(starts[b] <= k, 1, 0)
+            owners.append(jnp.where(k < total, who, -1))
+
+    def turn_tiles():
+        for s in range(slots):
+            at = (s % 2) * rows_per
+            for j in range(n_dev):
+                kvt[s // 2, j * LANES : (j + 1) * LANES, at : at + rows_per] = kv[
+                    s, :, j * LANES : (j + 1) * LANES
+                ].T
+
+    def image_part(acc, picks):
+        found = jnp.zeros((slots, rows_per), f32)
+        for s in range(0, slots, 2):
+            out = jnp.zeros((slots, 2 * rows_per), f32)
+            for picked, at in picks:
+                out = out + jnp.dot(picked, kvt[s // 2, at, :], preferred_element_type=f32)
+            found = jnp.where(slot_row == s, out[:, :rows_per], found)
+            found = jnp.where(slot_row == s + 1, out[:, rows_per:], found)
+        return found if acc is None else acc + found
 
     def image_of(acc):
-        high = acc.astype(bf16)
-        rest = acc - high.astype(f32)
-        mid = rest.astype(bf16)
-        low = (rest - mid.astype(f32)).astype(bf16)
-        image = jnp.zeros((blocks, rows_per), f32)
-        for term in (high, mid, low):
-            image = image + lax.dot_general(
-                owner_hot, term, (((1,), (1,)), ((), ())), preferred_element_type=f32
-            )
-        return image
-
-    def no_image():
-        return jnp.zeros((rows_per, slots), f32)
+        parts = [jnp.zeros((blocks, rows_per), f32) for _ in range(4)]
+        for s in range(slots):
+            term = jnp.where(block_row == owners[s], acc[s : s + 1, :], 0.0)
+            parts[s % 4] = parts[s % 4] + term
+        return (parts[0] + parts[1]) + (parts[2] + parts[3])
 
     def first_image():
         copies[0].wait()
@@ -413,11 +415,8 @@
             wide_col == lax.broadcasted_iota(i32, (32, n_cb), 1), 1.0, 0.0
         ).astype(bf16)
         picked = jnp.dot(own_hot, pbf[...], preferred_element_type=f32).astype(bf16)[:slots]
-        acc = no_image()
-        for c in range(n_chip):
-            lanes = slice(c * span, (c + 1) * span)
-            acc = image_part(acc, picked[:, lanes], lanes)
-        return image_of(acc)
+        spans = [slice(c * span, (c + 1) * span) for c in range(n_chip)]
+        return image_of(image_part(None, [(picked[:, at], at) for at in spans]))
 
     def build_hot():
         stat_bytes(0).wait_recv()
@@ -469,6 +468,8 @@
             send_stat(0)
             for u in order:
                 send_pieces(it, u)
+            find_owners()
+            turn_tiles()
             image = first_image()
             load_slices()
             build_hot()
@@ -528,14 +529,18 @@
                 out_primal.at[d], out_primal.at[d], p_send.at[0], p_recv.at[0], g, partner
             ).start()
 
-        acc = no_image()
-        for u in range(n_chip):
-            one = bbuf.at[it, 0, 0] if u == 0 else bbuf.at[it, u]
-            bytes_of(one, b_send.at[it], b_recv.at[it, u]).wait_recv()
-            picked = jnp.concatenate(
-                [bbuf[it, u, h].reshape(slots, LANES) for h in range(2)], axis=1
-            )
-            acc = image_part(acc, picked, chunk(u))
+        acc = None
+        for stage in stages:
+            picks = []
+            for u in stage:
+                one = bbuf.at[it, 0, 0] if u == 0 else bbuf.at[it, u]
+                bytes_of(one, b_send.at[it], b_recv.at[it, u]).wait_recv()
+            for u in stage:
+                picked = jnp.concatenate(
+                    [bbuf[it, u, h].reshape(slots, LANES) for h in range(2)], axis=1
+                )
+                picks.append((picked, chunk(u)))
+            acc = image_part(acc, picks)
         next_image = image_of(acc)
         sigma = step_scale * weight
         dual = jnp.maximum(dual + sigma * (bounds - (2.0 * next_image - image)), 0.0)
@@ -581,6 +586,28 @@
     bytes_of(out_primal.at[pl.ds(0, n_chip)], p_send.at[0], p_recv.at[0]).wait_recv()
 
 
+def place_kernel(slices, dual, weight, out_primal, out_dual, out_weight, flat, sem):
+    n_dev, n_cb, _ = slices.shape
+    copies = [
+        pltpu.make_async_copy(dual, out_dual, sem.at[4]),
+        pltpu.make_async_copy(weight, out_weight, sem.at[5]),
+    ]
+    for copy in copies:
+        copy.start()
+    part = n_cb // 4
+    for q in range(4):
+        for j in range(n_dev):
+            flat[pl.ds(q * part * n_dev + j, part, stride=n_dev), :] = slices[
+                j, q * part : (q + 1) * part, :
+            ]
+        here = pl.ds(q * part * n_dev, part * n_dev)
+        copy = pltpu.make_async_copy(flat.at[here], out_primal.at[here], sem.at[q])
+        copy.start()
+        copies.append(copy)
+    for copy in copies:
+        copy.wait()
+
+
 def split_device(mesh_shape, *args):
     tiles, cols, counts, dest, row_bounds, dual_start, primal, cost, upper = args
     slots, rows_per, width = tiles.shape
@@ -608,6 +635,7 @@
         out_specs=(vmem, vmem, vmem),
         scratch_shapes=[
             pltpu.VMEM((slots, rows_per, width), bf16),
+            pltpu.VMEM((slots // 2, width, 2 * rows_per), bf16),
             pltpu.VMEM(flat, f32),
             pltpu.VMEM(flat, f32),
             pltpu.VMEM(flat, f32),
@@ -664,8 +692,20 @@
             )
         )
     )
-    primal_final = out_primal.transpose(1, 0, 2).reshape(-1)
-    return primal_final, out_dual.reshape(-1), out_weight[0, :1]
+    primal_final, dual_final, weight_final = pl.pallas_call(
+        place_kernel,
+        name="pdhg_place",
+        out_shape=(
+            jax.ShapeDtypeStruct(flat, f32),
+            jax.ShapeDtypeStruct((n_dev, 1, rows_per), f32),
+            jax.ShapeDtypeStruct((1, LANES), f32),
+        ),
+        in_specs=[vmem] * 3,
+        out_specs=(far, far, far),
+        scratch_shapes=[pltpu.VMEM(flat, f32), dma((6,))],
+        compiler_params=pltpu.CompilerParams(vmem_limit_bytes=8 * 10**6),
+    )(*(pltpu.with_memory_space_constraint(x, pltpu.VMEM) for x in (out_primal, out_dual, out_weight)))
+    return primal_final.reshape(-1), dual_final.reshape(-1), weight_final[0, :1]
 
 
 def solution(mesh):

time: 50.9 us -> 46.4 us (0.912)
  local copies, waits for them, and re-layouts: 2.17 us -> 0 us
  between operations: 1.81 us -> 0.64 us
  Pallas kernels: 46.7 us -> 45.6 us
    pallas_call x1, Pallas kernels: 46.7 us -> 44.5 us  [split_device(): pl.pallas_call(functools.partial(split_kernel, n_grp, n_dev), name='pdhg_...]
    transpose x1 -> x0, local copies, waits for them, and re-layouts: 1.58 us -> none  [split_device(): primal_final = out_primal.transpose(1, 0, 2).reshape(-1)]
    pallas_call x0 -> x1, Pallas kernels: none -> 1.07 us  [split_device(): pl.pallas_call(place_kernel, name='pdhg_place', out_shape=(jax.ShapeDtype...]
    unnamed x1 -> x0, local copies, waits for them, and re-layouts: 0.59 us -> none
where the time goes in v5:
time: 46.4 us; the launch traced here: 46.2 us
  Pallas kernels  45.6 us (98%)
  between operations  0.64 us (1%)
    pallas_call x1, Pallas kernels, split_device(): pl.pallas_call(functools.partial(split_kernel, n_grp, n_dev), name='pdhg_...  44.5 us
    pallas_call x1, Pallas kernels, split_device(): pl.pallas_call(place_kernel, name='pdhg_place', out_shape=(jax.ShapeDtype...  1.07 us

profile of v5, /device:TPU:0, one launch (start us, length us, event | category | flops | bytes accessed | tf_op | source)
XLA Modules:
  0.0 46.2 jit_solution(4637256471750636391)
XLA Ops:
  0.6 44.5 %pdhg_split.1 = (f32[8,256,128]{2,1,0:T(8,128)S(1)}, f32[8,1,128]{2,1,0:T(1,128)S(1)}, f32[1,128]{1,0:T(1,128)S(1)}) custom-call(s32[20]{0:T(128)} %cols_in.1, s32[8]{0:T(128)} %counts_in.1, s32[8]{0:T(128)} %dest_in.1, bf16[8,128]{1,0:T(8,128)(2,1)} %bitcast.12, bf16[8,128]{1,0:T(8,128)(2,1)} %bitcast.13, bf16[20,128,1024]{2,1,0:T(8,128)(2,1)} %tiles.1, ...), custom_call_target="tpu_custom_call" | custom-call | tf_op jit(solution)/shard_map/pdhg_split/pallas_call | solution.py:626
  45.1 1.1 %pdhg_place.1 = (f32[2048,128]{1,0:T(8,128)}, f32[8,1,128]{2,1,0:T(1,128)}, f32[1,128]{1,0:T(1,128)}) custom-call(f32[8,256,128]{2,1,0:T(8,128)S(1)} %get-tuple-element.9.slices, f32[8,1,128]{2,1,0:T(1,128)S(1)} %get-tuple-element.10.dual, f32[1,128]{1,0:T(1,128)S(1)} %get-tuple-element.11.weight), custom_call_target="tpu_custom_call" | custom-call | tf_op jit(solution)/shard_map/pdhg_place/pallas_call | solution.py:695

commit v6 on v5

--- a/solution.py
+++ b/solution.py
@@ -107,7 +107,7 @@
 def fits(mesh_shape, slots, rows_per, width, blocks, column_blocks):
     n_grp, n_dev = mesh_shape["grp"], mesh_shape["dev"]
     n_chip = n_dev // 2
-    if n_dev % 2 or n_chip & (n_chip - 1) or n_grp & (n_grp - 1) or width != n_dev * LANES:
+    if n_dev % 2 or n_chip & (n_chip - 1) or n_grp != 4 or width != n_dev * LANES:
         return False
     if rows_per != LANES or blocks != n_dev or blocks != 8 or slots > 32:
         return False
@@ -148,6 +148,7 @@
     bsend,
     bbuf,
     stat,
+    shift,
     dsend,
     drecv,
     cols_at,
@@ -168,6 +169,8 @@
     f_recv,
     p_send,
     p_recv,
+    n_send,
+    n_recv,
     dual_send,
     dual_recv,
 ):
@@ -186,6 +189,11 @@
     twin = 1 - core
     partner = chip * 2 + twin
     me = g * n_dev + d
+    low_mid = n_grp // 2 - 1
+    near = jnp.where(g <= low_mid, low_mid, low_mid + 1)
+    away = n_grp - 1 - near
+    is_owner = g == near
+    beside = g ^ 1
 
     def remote(src, dst, ssem, rsem, tg, td):
         return pltpu.make_async_remote_copy(
@@ -230,6 +238,7 @@
         copy.start()
     order = [u for u in range(n_chip - 1, 0, -1)] + [0]
     planes = sorted(range(1, n_grp), key=lambda a: (-(a.bit_length()), a))
+    wide = ITERS - 1
     stages = [[0], [u for u in range(1, n_chip - 1)], [n_chip - 1]]
     part = 4
 
@@ -336,6 +345,20 @@
                 td,
             ).start()
 
+        if it < wide:
+            for h in range(2):
+                send(asend.at[it, u, h], away, (chip ^ u) * 2 + h)
+            if u:
+                for h in range(2):
+                    send(asend.at[it, u, h], near, (chip ^ u) * 2 + h)
+            else:
+                send(asend.at[it, 0, twin], near, partner)
+
+                @pl.when(jnp.logical_not(is_owner))
+                def _():
+                    send(asend.at[it, 0, core], near, d)
+
+            return
         for a in planes:
             for h in range(2):
                 send(asend.at[it, u, h], g ^ a, (chip ^ u) * 2 + h)
@@ -376,6 +399,11 @@
                 who = who + jnp.where(starts[b] <= k, 1, 0)
             owners.append(jnp.where(k < total, who, -1))
 
+    def back_sent(it):
+        most = bbuf.at[it, pl.ds(0, n_chip - 1)]
+        bytes_of(most, b_send.at[it], b_recv.at[it, 0]).wait_send()
+        bytes_of(bbuf.at[it, 0, 0], b_send.at[it], b_recv.at[it, 0]).wait_send()
+
     def turn_tiles():
         for s in range(slots):
             at = (s % 2) * rows_per
@@ -406,7 +434,11 @@
         for j in range(n_dev):
             value = pv[pl.ds(j, n_cb, stride=n_dev), :]
             pbf[:, j * LANES : (j + 1) * LANES] = value.astype(bf16)
-        pnow[...] = pv[pl.ds(d, n_cb, stride=n_dev), :]
+
+        @pl.when(is_owner)
+        def _():
+            pnow[...] = pv[pl.ds(d, n_cb, stride=n_dev), :]
+
         wide = lax.broadcasted_iota(i32, (32, n_cb), 0)
         wide_col = jnp.full((32, n_cb), -1, i32)
         for s in range(slots):
@@ -428,18 +460,20 @@
                 if high > 0 and low < LANES:
                     line = jnp.where((lane >= low) & (lane < high), stat[0, k], line)
             hot[:, t * LANES : (t + 1) * LANES] = jnp.where(block_of == line, 1.0, 0.0).astype(bf16)
-        back = n_dev * slots
+        back = 2 * n_dev * slots
         back_row = lax.broadcasted_iota(i32, (back, LANES), 0)
         back_lane = lax.broadcasted_iota(i32, (back, LANES), 1)
         back_dev, back_slot = back_row // slots, back_row % slots
         found = jnp.zeros((back, LANES), f32)
-        for u in range(n_chip):
-            for h in range(2):
-                src = g * n_dev + (chip ^ u) * 2 + h
-                shift = (src * slots) % LANES
-                at = jnp.where(back_lane < shift, back_lane - shift + LANES, back_lane - shift)
-                hit = (back_dev == u * 2 + h) & (at == back_slot)
-                found = jnp.where(hit, stat[0, src] + 1.0, found)
+        for w in range(2):
+            for u in range(n_chip):
+                for h in range(2):
+                    src = (g ^ w) * n_dev + (chip ^ u) * 2 + h
+                    turned = (src * slots) % LANES
+                    at = back_lane - turned
+                    at = jnp.where(at < 0, at + LANES, at)
+                    hit = (back_dev == w * n_dev + u * 2 + h) & (at == back_slot)
+                    found = jnp.where(hit, stat[0, src] + 1.0, found)
         wanted = jnp.sum(found, axis=1, keepdims=True) - 1.0
         lane_cb = lax.broadcasted_iota(i32, (back, n_cb), 1).astype(f32)
         hot_back[...] = jnp.where(wanted == lane_cb, 1.0, 0.0).astype(bf16)
@@ -451,6 +485,8 @@
         us[...] = uv[pl.ds(d, n_cb, stride=n_dev), :]
 
     weight = jnp.ones((1, 1), f32)
+    shift[...] = jnp.zeros((1, LANES), f32)
+    moved_rows = slice(low_mid * n_dev, (low_mid + 1) * n_dev)
     image = None
     for it in range(ITERS):
         if it == 0:
@@ -485,37 +521,61 @@
             send_pieces(it, sent_before[-1])
             stat_bytes(it).wait_recv()
             violation = jnp.sum(stat[it], axis=0)[:, LANES - 1 :]
-            change = jnp.sum(stat[it, 0:n_dev], axis=0)[:, :1]
+            change = jnp.sum(stat[it, moved_rows], axis=0)[:, :1]
             weight = jnp.sqrt(weight * jnp.sqrt((violation + 1e-06) / (change + 1e-06)))
         tau = step_scale / weight
-        piece_bytes(it).wait_recv()
-        grad = jnp.dot(
-            hot[...],
-            abuf.at[it].reshape(n_all * slots, LANES)[...],
-            preferred_element_type=f32,
-        )
-        old = pnow[...]
-        new = jnp.minimum(jnp.maximum(old - tau * (cs[...] - grad), 0.0), us[...])
-        back = jnp.dot(hot_back[...], new.astype(bf16), preferred_element_type=f32)
-        back = back.astype(bf16).reshape(n_chip, 2, packs, TILE, LANES)
-        bsend[it] = back
-        bbuf[it, 0, core] = jnp.where(core == 0, back[0, 0], back[0, 1])
-
-        def send_back(src, dst, u, td):
-            remote(src, dst, b_send.at[it], b_recv.at[it, u], g, td).start()
-
-        for u in order[:-1]:
-            for h in range(2):
-                send_back(
-                    bsend.at[it, u, h], bbuf.at[it, u, core], u, (chip ^ u) * 2 + h
-                )
-        send_back(bsend.at[it, 0, twin], bbuf.at[it, 0, core], 0, partner)
-        gap = new - old
-        moved = jnp.sum(gap * gap, axis=(0, 1), keepdims=True)
-        if it < ITERS - 1:
-            pnow[...] = new
+        def step():
+            grad = jnp.dot(
+                hot[...],
+                abuf.at[it].reshape(n_all * slots, LANES)[...],
+                preferred_element_type=f32,
+            )
+            old = pnow[...]
+            new = jnp.minimum(jnp.maximum(old - tau * (cs[...] - grad), 0.0), us[...])
+            rounded = new.astype(bf16)
+            for w in (1, 0) if it < wide else (0,):
+                rows_here = slice(w * n_dev * slots, (w + 1) * n_dev * slots)
+                back = jnp.dot(hot_back[rows_here], rounded, preferred_element_type=f32)
+                back = back.astype(bf16).reshape(n_chip, 2, packs, TILE, LANES)
+                bsend[it, w] = back
+                if w == 0:
+                    bbuf[it, 0, core] = jnp.where(core == 0, back[0, 0], back[0, 1])
+                for u in order:
+                    for h in range(2):
+                        if w or u:
+                            send_back(w, u, h, (chip ^ u) * 2 + h)
+                if w == 0:
+                    send_back(0, 0, twin, partner)
+            gap = new - old
+            moved = jnp.sum(gap * gap, axis=(0, 1), keepdims=True)
+            shift[...] = jnp.broadcast_to(moved, (1, LANES))
+            return new
+
+        def send_back(w, u, h, td):
+            remote(
+                bsend.at[it, w, u, h],
+                bbuf.at[it, u, core],
+                b_send.at[it],
+                b_recv.at[it, u],
+                g ^ w,
+                td,
+            ).start()
+
+        if it < wide:
+
+            @pl.when(is_owner)
+            def _():
+                piece_bytes(it).wait_recv()
+                pnow[...] = step()
+
         else:
-            out_primal[d] = new
+            piece_bytes(it).wait_recv()
+
+            @pl.when(jnp.logical_not(is_owner))
+            def _():
+                bytes_of(pnow, n_send.at[0], n_recv.at[0]).wait_recv()
+
+            out_primal[d] = step()
             for u in order[:-1]:
                 remote(
                     out_primal.at[d],
@@ -533,21 +593,38 @@
         for stage in stages:
             picks = []
             for u in stage:
-                one = bbuf.at[it, 0, 0] if u == 0 else bbuf.at[it, u]
-                bytes_of(one, b_send.at[it], b_recv.at[it, u]).wait_recv()
+                if u == 0 and it < wide:
+
+                    @pl.when(is_owner)
+                    def _():
+                        bytes_of(bbuf.at[it, 0, 0], b_send.at[it], b_recv.at[it, 0]).wait_recv()
+
+                    @pl.when(jnp.logical_not(is_owner))
+                    def _():
+                        bytes_of(bbuf.at[it, 0], b_send.at[it], b_recv.at[it, 0]).wait_recv()
+
+                else:
+                    one = bbuf.at[it, u] if u else bbuf.at[it, 0, 0]
+                    bytes_of(one, b_send.at[it], b_recv.at[it, u]).wait_recv()
             for u in stage:
                 picked = jnp.concatenate(
                     [bbuf[it, u, h].reshape(slots, LANES) for h in range(2)], axis=1
                 )
                 picks.append((picked, chunk(u)))
             acc = image_part(acc, picks)
+            if it == wide - 1 and stage == stages[0]:
+
+                @pl.when(is_owner)
+                def _():
+                    remote(pnow, pnow, n_send.at[0], n_recv.at[0], beside, d).start()
+
         next_image = image_of(acc)
         sigma = step_scale * weight
         dual = jnp.maximum(dual + sigma * (bounds - (2.0 * next_image - image)), 0.0)
         short = jnp.maximum(bounds - next_image, 0.0)
         image = next_image
         missed = jnp.sum(short * short, axis=(0, 1), keepdims=True)
-        stat[it + 1, me] = jnp.where(lane < LANES // 2, moved, missed)
+        stat[it + 1, me] = jnp.where(lane < LANES // 2, shift[...], missed)
         send_stat(it + 1)
 
     for e in range(n_dev):
@@ -569,15 +646,29 @@
     out_dual[...] = drecv[...]
     stat_bytes(ITERS).wait_recv()
     violation = jnp.sum(stat[ITERS], axis=0)[:, LANES - 1 :]
-    change = jnp.sum(stat[ITERS, 0:n_dev], axis=0)[:, :1]
+    change = jnp.sum(stat[ITERS, moved_rows], axis=0)[:, :1]
     weight = jnp.sqrt(weight * jnp.sqrt((violation + 1e-06) / (change + 1e-06)))
     out_weight[...] = jnp.broadcast_to(weight, (1, LANES))
-    for it in range(ITERS):
-        piece_bytes(it).wait_send()
-        bytes_of(
-            bbuf.at[it, pl.ds(0, n_chip - 1)], b_send.at[it], b_recv.at[it, 0]
-        ).wait_send()
-        bytes_of(bbuf.at[it, 0, 0], b_send.at[it], b_recv.at[it, 0]).wait_send()
+    for it in range(wide):
+        sends = 2 * n_dev - 1
+        bytes_of(abuf.at[it, pl.ds(0, sends * packs)], a_send.at[it], a_recv.at[it]).wait_send()
+
+        @pl.when(jnp.logical_not(is_owner))
+        def _():
+            bytes_of(abuf.at[it, pl.ds(0, packs)], a_send.at[it], a_recv.at[it]).wait_send()
+
+        @pl.when(is_owner)
+        def _():
+            bytes_of(bsend.at[it, 1], b_send.at[it], b_recv.at[it, 0]).wait_send()
+            back_sent(it)
+
+    piece_bytes(wide).wait_send()
+    back_sent(wide)
+
+    @pl.when(is_owner)
+    def _():
+        bytes_of(pnow, n_send.at[0], n_recv.at[0]).wait_send()
+
     for turn_no in range(ITERS + 1):
         stat_bytes(turn_no).wait_send()
     bytes_of(drecv.at[pl.ds(0, n_dev - 1)], dual_send.at[0], dual_recv.at[0]).wait_send()
@@ -644,12 +735,13 @@
             pltpu.VMEM((n_cb, LANES), f32),
             pltpu.VMEM((n_cb, width), bf16),
             pltpu.VMEM((n_cb, n_all * slots), bf16),
-            pltpu.VMEM((n_dev * slots, n_cb), bf16),
+            pltpu.VMEM((2 * n_dev * slots, n_cb), bf16),
             pltpu.VMEM((ITERS, n_chip, 2, packs, TILE, LANES), bf16),
             pltpu.VMEM((ITERS, n_all * packs, TILE, LANES), bf16),
-            pltpu.VMEM((ITERS, n_chip, 2, packs, TILE, LANES), bf16),
+            pltpu.VMEM((ITERS, 2, n_chip, 2, packs, TILE, LANES), bf16),
             pltpu.VMEM((ITERS, n_chip, 2, packs, TILE, LANES), bf16),
             pltpu.VMEM((ITERS + 1, n_all, 1, LANES), f32),
+            pltpu.VMEM((1, LANES), f32),
             pltpu.VMEM((n_dev, 1, rows_per), f32),
             pltpu.VMEM((n_dev, 1, rows_per), f32),
             pltpu.SMEM((slots,), jnp.int32),
@@ -668,6 +760,8 @@
             dma((ITERS + 1,)),
             dma((1,)),
             dma((n_chip,)),
+            dma((1,)),
+            dma((1,)),
             dma((1,)),
             dma((1,)),
             dma((1,)),

time: 46.4 us -> 45.6 us (0.983)
  Pallas kernels: 45.6 us -> 44.7 us
    pallas_call x1, Pallas kernels: 44.5 us -> 43.7 us  [split_device(): pl.pallas_call(functools.partial(split_kernel, n_grp, n_dev), name='pdhg_...]
where the time goes in v6:
time: 45.6 us; the launch traced here: 45.4 us
  Pallas kernels  44.7 us (98%)
  between operations  0.64 us (1%)
    pallas_call x1, Pallas kernels, split_device(): pl.pallas_call(functools.partial(split_kernel, n_grp, n_dev), name='pdhg_...  43.7 us
    pallas_call x1, Pallas kernels, split_device(): pl.pallas_call(place_kernel, name='pdhg_place', out_shape=(jax.ShapeDtype...  1.07 us

profile of v6, /device:TPU:0, one launch (start us, length us, event | category | flops | bytes accessed | tf_op | source)
XLA Modules:
  0.0 45.4 jit_solution(7969555455784997343)
XLA Ops:
  0.6 43.7 %pdhg_split.1 = (f32[8,256,128]{2,1,0:T(8,128)S(1)}, f32[8,1,128]{2,1,0:T(1,128)S(1)}, f32[1,128]{1,0:T(1,128)S(1)}) custom-call(s32[20]{0:T(128)} %cols_in.1, s32[8]{0:T(128)} %counts_in.1, s32[8]{0:T(128)} %dest_in.1, bf16[8,128]{1,0:T(8,128)(2,1)} %bitcast.12, bf16[8,128]{1,0:T(8,128)(2,1)} %bitcast.13, bf16[20,128,1024]{2,1,0:T(8,128)(2,1)} %tiles.1, ...), custom_call_target="tpu_custom_call" | custom-call | tf_op jit(solution)/shard_map/pdhg_split/pallas_call | solution.py:717
  44.3 1.1 %pdhg_place.1 = (f32[2048,128]{1,0:T(8,128)}, f32[8,1,128]{2,1,0:T(1,128)}, f32[1,128]{1,0:T(1,128)}) custom-call(f32[8,256,128]{2,1,0:T(8,128)S(1)} %get-tuple-element.9.slices, f32[8,1,128]{2,1,0:T(1,128)S(1)} %get-tuple-element.10.dual, f32[1,128]{1,0:T(1,128)S(1)} %get-tuple-element.11.weight), custom_call_target="tpu_custom_call" | custom-call | tf_op jit(solution)/shard_map/pdhg_place/pallas_call | solution.py:789
